TPU v7x, 32 devices: a 4x4x1 block of a 4x4x8 slice. The times are simulated.
32 devices in a mesh: dp: 1 (over z), tp: 4 (over y), fsdp: 8 (over x, core).
Axes of the slice: x: 4, y: 4, z: 1, core: 2. Of those that a mesh axis runs over, the one named last changes fastest.
The devices are a block of a 4x4x8 slice.
Arguments:
- hidden: bfloat16 [64, 512, 2048], P(('dp', 'fsdp'))
- seq_lens: int32 [64], P(('dp', 'fsdp'))
- w_qkv: bfloat16 [2, 2048, 3, 32, 64], P(None, 'fsdp', None, 'tp')
- b_qkv: bfloat16 [2, 3, 2048], P(None, None, ('tp', 'fsdp'))
- w_proj: bfloat16 [2, 2048, 2048], P(None, ('tp', 'fsdp'))
- w_up: bfloat16 [2, 2048, 8192], P(None, 'fsdp', 'tp')
- b_up: bfloat16 [2, 8192], P(None, ('tp', 'fsdp'))
- w_down: bfloat16 [2, 8192, 2048], P(None, ('tp', 'fsdp'))
- b_resid: bfloat16 [2, 2, 2048], P(None, None, 'fsdp')
- ln_params: float32 [2, 4, 2048], P(None, None, 'fsdp')
Outputs:
- output: bfloat16 [64, 512, 2048], P(('dp', 'fsdp'))
All inputs are finite; a program needn't handle non-finite values.
Results may differ from a plain program's by a relative error of at most 0.0175426.
Values are sent between devices in bfloat16 or wider.
A program may use at most 768 MiB of HBM per device.

v0:
```python
import jax
import jax.numpy as jnp
from jax import lax
from jax.sharding import PartitionSpec as P


def layer_norm(acts_in, ln_gain, ln_shift):
    as_f32 = acts_in.astype(jnp.float32)
    row_mean = jnp.mean(as_f32, axis=-1, keepdims=True)
    centered = as_f32 - row_mean
    row_var = jnp.mean(centered * centered, axis=-1, keepdims=True)
    return (centered * lax.rsqrt(row_var + 1e-5) * ln_gain + ln_shift).astype(jnp.bfloat16)


def attend(qkv_out, allowed):
    head_dim = qkv_out.shape[-1]
    scores = jnp.einsum('bqhe,bkhe->bhqk', qkv_out[:, :, 0], qkv_out[:, :, 1], preferred_element_type=jnp.float32) * head_dim ** -0.5
    scores = jnp.where(allowed, scores, -1e30)
    attn_probs = jax.nn.softmax(scores, axis=-1).astype(jnp.bfloat16)
    return jnp.einsum('bhqk,bkhe->bqhe', attn_probs, qkv_out[:, :, 2], preferred_element_type=jnp.float32).astype(jnp.bfloat16)


def solution(mesh):
    rows_spec = P(('dp', 'fsdp'), None, None)
    in_specs = (rows_spec, P(('dp', 'fsdp')), P(None, 'fsdp', None, 'tp', None), P(None, None, ('tp', 'fsdp')), P(None, ('tp', 'fsdp'), None), P(None, 'fsdp', 'tp'), P(None, ('tp', 'fsdp')), P(None, ('tp', 'fsdp'), None), P(None, None, 'fsdp'), P(None, None, 'fsdp'))

    def per_device(hidden, seq_lens, w_qkv, b_qkv, w_proj, w_up, b_up, w_down, b_resid, ln_params):
        n_layers = w_qkv.shape[0]
        local_heads = w_qkv.shape[3]
        head_dim = w_qkv.shape[4]
        seq_len = hidden.shape[1]
        positions = jnp.arange(seq_len)
        allowed = ((positions[None, None, :] <= positions[None, :, None]) & (positions[None, None, :] < seq_lens[:, None, None]))[:, None]
        current = hidden
        for layer_idx in range(n_layers):
            qkv_full = lax.all_gather(w_qkv[layer_idx], 'fsdp', axis=0, tiled=True)
            qkv_bias = lax.all_gather(b_qkv[layer_idx], 'fsdp', axis=1, tiled=True).reshape(3, local_heads, head_dim).astype(jnp.float32)
            proj_full = lax.all_gather(w_proj[layer_idx], 'fsdp', axis=0, tiled=True).reshape(local_heads, head_dim, -1)
            up_full = lax.all_gather(w_up[layer_idx], 'fsdp', axis=0, tiled=True)
            up_bias = lax.all_gather(b_up[layer_idx], 'fsdp', axis=0, tiled=True).astype(jnp.float32)
            down_full = lax.all_gather(w_down[layer_idx], 'fsdp', axis=0, tiled=True)
            resid_bias = lax.all_gather(b_resid[layer_idx], 'fsdp', axis=1, tiled=True).astype(jnp.float32)
            ln_full = lax.all_gather(ln_params[layer_idx], 'fsdp', axis=1, tiled=True)
            normed = layer_norm(current, ln_full[0], ln_full[1])
            qkv_out = (jnp.einsum('bsd,dkhe->bskhe', normed, qkv_full, preferred_element_type=jnp.float32) + qkv_bias).astype(jnp.bfloat16)
            context = attend(qkv_out, allowed)
            attn_part = jnp.einsum('crif,ife->cre', context, proj_full, preferred_element_type=jnp.float32).astype(jnp.bfloat16)
            attn_sum = lax.psum(attn_part, 'tp')
            mid_state = (current.astype(jnp.float32) + attn_sum.astype(jnp.float32) + resid_bias[0]).astype(jnp.bfloat16)
            normed_mid = layer_norm(mid_state, ln_full[2], ln_full[3])
            up_out = jnp.einsum('bsd,df->bsf', normed_mid, up_full, preferred_element_type=jnp.float32) + up_bias
            hidden_up = jnp.maximum(up_out, 0.0).astype(jnp.bfloat16)
            down_part = jnp.einsum('bsf,fd->bsd', hidden_up, down_full, preferred_element_type=jnp.float32).astype(jnp.bfloat16)
            down_sum = lax.psum(down_part, 'tp')
            current = (mid_state.astype(jnp.float32) + down_sum.astype(jnp.float32) + resid_bias[1]).astype(jnp.bfloat16)
        return current

    return jax.shard_map(per_device, mesh=mesh, in_specs=in_specs, out_specs=rows_spec, check_vma=False)
```

profile of v0, /device:TPU:97, one launch (start us, length us, event | category | flops | bytes accessed | tf_op | source)
XLA Modules:
  0.0 1805.3 jit_solution(5793083290300593245)
XLA Ops:
  6.6 2.7 fusion.97
  9.4 1.9 fusion.98
  11.5 1.3 fusion.102
  12.8 20.8 %all-gather = f32[1,4,2048]{2,1,0:T(4,128)S(1)} all-gather(f32[1,4,256]{2,1,0:T(4,128)S(1)} %get-tuple-element.30), channel_id=2, replica_groups=mesh['dp'=1,'tp'=4,'fsdp'=8] {'fsdp'}, dimensions={2}, use_global_device_ids=true | all-gather | bytes 36864 | tf_op jit(solution)/shard_map/all_gather | solution.py:43
  33.5 0.6 fusion.100
  34.2 1.3 fusion.105
  35.5 0.1 copy.29
  35.6 22.0 %all-gather.2 = bf16[1,3,512]{1,0,2:T(2,128)(2,1)S(1)} all-gather(bf16[1,3,64]{1,0,2:T(2,128)(2,1)S(1)} %copy.29), channel_id=4, replica_groups=mesh['dp'=1,'tp'=4,'fsdp'=8] {'fsdp'}, dimensions={2}, use_global_device_ids=true | all-gather | bytes 3456 | tf_op jit(solution)/shard_map/all_gather | solution.py:37
  57.6 0.2 copy.18
  57.9 8.5 convert_reduce_fusion.3
  66.4 2.2 copy-done
  68.5 5.5 fusion.24
  74.1 1.2 broadcast_and_fusion
  75.4 35.4 %add_convert_fusion.1 = bf16[8,512,3,8,64]{1,4,3,2,0:T(8,128)(2,1)} fusion(f32[3,8,64]{2,1,0:T(8,128)S(1)} %reshape.127, bf16[8,512,2048]{2,1,0:T(8,128)(2,1)} %param.10, f32[2048]{0:T(1024)S(1)} %bitcast.156, f32[2048]{0:T(1024)S(1)} %bitcast.157, f32[8,512]{1,0:T(8,128)S(1)} %add_rsqrt_fusion.3, f32[8,512]{1,0:T(8,128)S(1)} %broadcast_multiply_fusion.3, ...), kind=kOutput, calls=%fused_computation.67 | convolution fusion | flops 25832718336 | bytes 35706880 | tf_op jit(solution)/shard_map/bsd,dkhe->bskhe/dot_general | solution.py:45
  110.9 32.3 %fusion.107 = (f32[8,8,512]{2,1,0:T(8,128)S(1)}, f32[8,8,512,512]{2,3,1,0:T(8,128)}) fusion(pred[8,512,512]{1,2,0:T(8,128)(4,1)S(1)} %broadcast_and_fusion, bf16[8,512,3,8,64]{1,4,3,2,0:T(8,128)(2,1)} %add_convert_fusion.1), kind=kOutput, calls=%fused_computation.139 | convolution fusion | flops 2214593024 | bytes 77725696 | tf_op jit(solution)/shard_map/sub | solution.py:19
  143.2 25.3 %fusion.118 = bf16[8,512,8,64]{1,3,2,0:T(8,128)(2,1)} fusion(f32[8,8,512,512]{2,3,1,0:T(8,128)} %get-tuple-element.40, f32[8,8,512]{2,1,0:T(8,128)S(1)} %get-tuple-element.39, bf16[8,512,3,8,64]{1,4,3,2,0:T(8,128)(2,1)} %add_convert_fusion.1), kind=kOutput, calls=%fused_computation.105.clone | convolution fusion | flops 2183135232 | bytes 75628544 | tf_op jit(solution)/shard_map/bhqk,bkhe->bqhe/dot_general | solution.py:20
  168.4 15.1 bitcast_convert_fusion.1
  183.6 1.4 copy-done.6
  185.1 1.5 fusion.96
  186.7 3.2 fusion.95
  190.0 0.5 fusion.106
  190.5 21.7 %all-gather.6 = bf16[1,2048]{1,0:T(2,128)(2,1)S(1)} all-gather(bf16[1,256]{1,0:T(2,128)(2,1)S(1)} %get-tuple-element.38), channel_id=8, replica_groups=mesh['dp'=1,'tp'=4,'fsdp'=8] {'fsdp'}, dimensions={1}, use_global_device_ids=true | all-gather | bytes 4608 | tf_op jit(solution)/shard_map/all_gather | solution.py:40
  212.3 0.5 fusion.104
  212.9 23.2 %all-gather.4 = bf16[1,2,2048]{2,1,0:T(2,128)(2,1)S(1)} all-gather(bf16[1,2,256]{2,1,0:T(2,128)(2,1)S(1)} %get-tuple-element.33), channel_id=6, replica_groups=mesh['dp'=1,'tp'=4,'fsdp'=8] {'fsdp'}, dimensions={2}, use_global_device_ids=true | all-gather | bytes 9216 | tf_op jit(solution)/shard_map/all_gather | solution.py:42
  236.1 0.6 fusion.103
  236.7 242.9 %all-reduce.5.cloned.1.call-done = bf16[8,512,2048]{2,1,0:T(8,128)(2,1)} async-done(((bf16[8,512,2048]{2,1,0:T(8,128)(2,1)}), bf16[8,512,2048]{2,1,0:T(8,128)(2,1)}) %all-reduce.5.cloned.1.call-update) | async-done | bytes 16777232 | tf_op jit(solution)/shard_map/psum | solution.py:48
  479.5 14.2 convert_reduce_fusion.2
  493.8 6.1 copy-done.1
  499.9 5.5 fusion.20
  505.4 23.1 %all-gather.29.cloned.1.call-done = bf16[1,2048,2048]{2,1,0:T(8,128)(2,1)} async-done(((bf16[1,256,2048]{2,1,0:T(8,128)(2,1)}), bf16[1,2048,2048]{2,1,0:T(8,128)(2,1)}) %all-gather.29.cloned.1.call-update) | async-done | bytes 8388624 | tf_op jit(solution)/shard_map/all_gather | solution.py:39
  528.5 42.0 %maximum_convert_fusion.1 = bf16[8,512,2048]{2,1,0:T(8,128)(2,1)} fusion(bf16[8,512,2048]{2,1,0:T(8,128)(2,1)} %copy-done.1, f32[2048]{0:T(1024)S(1)} %bitcast.148, f32[2048]{0:T(1024)S(1)} %bitcast.151, f32[2048]{0:T(1024)S(1)} %bitcast.150, f32[8,512]{1,0:T(8,128)S(1)} %add_rsqrt_fusion.2, f32[8,512]{1,0:T(8,128)S(1)} %broadcast_multiply_fusion.2, ...), kind=kOutput, calls=%fused_computation.57 | convolution fusion | flops 34435235840 | bytes 42000384 | tf_op jit(solution)/shard_map/bsd,df->bsf/dot_general | solution.py:51
  570.5 6.7 all-gather.31.cloned.1.call-done
  577.2 41.4 %convolution_convert_fusion.1 = bf16[8,512,2048]{2,1,0:T(8,128)(2,1)} fusion(bf16[8,512,2048]{2,1,0:T(8,128)(2,1)} %maximum_convert_fusion.1, bf16[1,2048,2048]{2,1,0:T(8,128)(2,1)} %all-gather.31.cloned.1.call-done), kind=kOutput, calls=%fused_computation.89 | convolution fusion | flops 34368126976 | bytes 41943040 | tf_op jit(solution)/shard_map/bsf,fd->bsd/dot_general | solution.py:53
  618.8 0.7 all-gather.33.cloned.1.call-update
  619.6 0.7 all-gather.35.cloned.1.call-update
  620.4 17.4 all-gather.8
  637.8 0.6 fusion.99
  638.5 0.1 copy.30
  638.6 22.3 %all-gather.10 = bf16[1,3,512]{1,0,2:T(2,128)(2,1)S(1)} all-gather(bf16[1,3,64]{1,0,2:T(2,128)(2,1)S(1)} %copy.30), channel_id=12, replica_groups=mesh['dp'=1,'tp'=4,'fsdp'=8] {'fsdp'}, dimensions={2}, use_global_device_ids=true | all-gather | bytes 3456 | tf_op jit(solution)/shard_map/all_gather | solution.py:37
  660.9 0.2 copy.21
  661.1 247.5 %all-reduce.7.cloned.1.call-done = bf16[8,512,2048]{2,1,0:T(8,128)(2,1)} async-done(((bf16[8,512,2048]{2,1,0:T(8,128)(2,1)}), bf16[8,512,2048]{2,1,0:T(8,128)(2,1)}) %all-reduce.7.cloned.1.call-update) | async-done | bytes 16777232 | tf_op jit(solution)/shard_map/psum | solution.py:54
  908.6 14.2 convert_reduce_fusion.1
  922.8 6.1 copy-done.2
  929.0 5.5 fusion.16
  934.5 17.5 all-gather.33.cloned.1.call-done
  952.0 34.9 %add_convert_fusion = bf16[8,512,3,8,64]{1,4,3,2,0:T(8,128)(2,1)} fusion(f32[3,8,64]{2,1,0:T(8,128)S(1)} %reshape.128, bf16[8,512,2048]{2,1,0:T(8,128)(2,1)} %copy-done.2, f32[2048]{0:T(1024)S(1)} %bitcast.154, f32[2048]{0:T(1024)S(1)} %bitcast.155, f32[8,512]{1,0:T(8,128)S(1)} %add_rsqrt_fusion.1, f32[8,512]{1,0:T(8,128)S(1)} %broadcast_multiply_fusion.1, ...), kind=kOutput, calls=%fused_computation.66 | convolution fusion | flops 25832718336 | bytes 35706880 | tf_op jit(solution)/shard_map/bsd,dkhe->bskhe/dot_general | solution.py:45
  986.9 32.3 %fusion.108 = (f32[8,8,512]{2,1,0:T(8,128)S(1)}, f32[8,8,512,512]{2,3,1,0:T(8,128)}) fusion(pred[8,512,512]{1,2,0:T(8,128)(4,1)S(1)} %copy-done.5, bf16[8,512,3,8,64]{1,4,3,2,0:T(8,128)(2,1)} %add_convert_fusion), kind=kOutput, calls=%fused_computation.140 | convolution fusion | flops 2214593024 | bytes 77725696 | tf_op jit(solution)/shard_map/sub | solution.py:19
  1019.2 25.3 %fusion.116 = bf16[8,512,8,64]{1,3,2,0:T(8,128)(2,1)} fusion(f32[8,8,512,512]{2,3,1,0:T(8,128)} %get-tuple-element.42, f32[8,8,512]{2,1,0:T(8,128)S(1)} %get-tuple-element.41, bf16[8,512,3,8,64]{1,4,3,2,0:T(8,128)(2,1)} %add_convert_fusion), kind=kOutput, calls=%fused_computation.104.clone.1 | convolution fusion | flops 2183135232 | bytes 75628544 | tf_op jit(solution)/shard_map/bhqk,bkhe->bqhe/dot_general | solution.py:20
  1044.5 14.9 bitcast_convert_fusion
  1059.5 0.6 all-gather.37.cloned.1.call-update
  1060.2 0.7 all-gather.39.cloned.1.call-update
  1061.0 18.5 %all-gather.14 = bf16[1,2048]{1,0:T(2,128)(2,1)S(1)} all-gather(bf16[1,256]{1,0:T(2,128)(2,1)S(1)} %copy-done.16), channel_id=16, replica_groups=mesh['dp'=1,'tp'=4,'fsdp'=8] {'fsdp'}, dimensions={1}, use_global_device_ids=true | all-gather | bytes 4608 | tf_op jit(solution)/shard_map/all_gather | solution.py:40
  1079.5 22.0 %all-gather.12 = bf16[1,2,2048]{2,1,0:T(2,128)(2,1)S(1)} all-gather(bf16[1,2,256]{2,1,0:T(2,128)(2,1)S(1)} %copy-done.17), channel_id=14, replica_groups=mesh['dp'=1,'tp'=4,'fsdp'=8] {'fsdp'}, dimensions={2}, use_global_device_ids=true | all-gather | bytes 9216 | tf_op jit(solution)/shard_map/all_gather | solution.py:42
  1101.5 0.6 fusion.101
  1102.1 247.9 %all-reduce.9.cloned.1.call-done = bf16[8,512,2048]{2,1,0:T(8,128)(2,1)} async-done(((bf16[8,512,2048]{2,1,0:T(8,128)(2,1)}), bf16[8,512,2048]{2,1,0:T(8,128)(2,1)}) %all-reduce.9.cloned.1.call-update) | async-done | bytes 16777232 | tf_op jit(solution)/shard_map/psum | solution.py:48
  1350.0 14.2 convert_reduce_fusion
  1364.3 6.1 copy-done.3
  1370.4 5.5 fusion.12
  1375.9 23.1 %all-gather.37.cloned.1.call-done = bf16[1,2048,2048]{2,1,0:T(8,128)(2,1)} async-done(((bf16[1,256,2048]{2,1,0:T(8,128)(2,1)}), bf16[1,2048,2048]{2,1,0:T(8,128)(2,1)}) %all-gather.37.cloned.1.call-update) | async-done | bytes 8388624 | tf_op jit(solution)/shard_map/all_gather | solution.py:39
  1399.0 42.0 %maximum_convert_fusion = bf16[8,512,2048]{2,1,0:T(8,128)(2,1)} fusion(bf16[8,512,2048]{2,1,0:T(8,128)(2,1)} %copy-done.3, f32[2048]{0:T(1024)S(1)} %bitcast.149, f32[2048]{0:T(1024)S(1)} %bitcast.153, f32[2048]{0:T(1024)S(1)} %bitcast.152, f32[8,512]{1,0:T(8,128)S(1)} %add_rsqrt_fusion, f32[8,512]{1,0:T(8,128)S(1)} %broadcast_multiply_fusion, ...), kind=kOutput, calls=%fused_computation.56 | convolution fusion | flops 34435235840 | bytes 42000384 | tf_op jit(solution)/shard_map/bsd,df->bsf/dot_general | solution.py:51
  1441.0 6.8 all-gather.39.cloned.1.call-done
  1447.8 41.4 %convolution_convert_fusion = bf16[8,512,2048]{2,1,0:T(8,128)(2,1)} fusion(bf16[8,512,2048]{2,1,0:T(8,128)(2,1)} %maximum_convert_fusion, bf16[1,2048,2048]{2,1,0:T(8,128)(2,1)} %all-gather.39.cloned.1.call-done), kind=kOutput, calls=%fused_computation.88 | convolution fusion | flops 34368126976 | bytes 41943040 | tf_op jit(solution)/shard_map/bsf,fd->bsd/dot_general | solution.py:53
  1489.3 289.9 %all-reduce.11.cloned.1.call-done = bf16[8,512,2048]{2,1,0:T(8,128)(2,1)} async-done(((bf16[8,512,2048]{2,1,0:T(8,128)(2,1)}), bf16[8,512,2048]{2,1,0:T(8,128)(2,1)}) %all-reduce.11.cloned.1.call-update) | async-done | bytes 16777232 | tf_op jit(solution)/shard_map/psum | solution.py:54
  1779.3 18.8 %fusion.35 = bf16[8,512,2048]{2,1,0:T(8,128)(2,1)} fusion(bf16[8,512,2048]{2,1,0:T(8,128)(2,1)} %copy-done.3, bf16[8,512,2048]{2,1,0:T(8,128)(2,1)} %all-reduce.11.cloned.1.call-done, f32[2048]{0:T(1024)S(1)} %bitcast.147), kind=kLoop, calls=%fused_computation.53 | loop fusion | flops 41943040 | bytes 50339840 | tf_op jit(solution)/shard_map/convert_element_type | solution.py:55
  (74 shorter events, 1.7 us)
Async XLA Ops:
  6.5 68.9 %all-gather.25.cloned.1.call-start = ((), (), s32[]{:S(2)}) async-start(), calls=%async_computation.4 | async-start | bytes 7077888 | tf_op jit(solution)/shard_map/all_gather | solution.py:36
  9.3 159.1 %all-gather.27.cloned.1.call-start = ((), (), s32[]{:S(2)}) async-start(), calls=%async_computation.5 | async-start | bytes 2359296 | tf_op jit(solution)/shard_map/all_gather | solution.py:38
  11.3 468.2 %all-reduce.5.cloned.1.call-start = ((), (), s32[]{:S(2)}) async-start(), calls=%async_computation | async-start | bytes 33554432 | tf_op jit(solution)/shard_map/psum | solution.py:48
  57.9 10.7 copy-start
  57.9 16.2 copy-start.19
  75.4 35.5 %copy-start.4 = (pred[8,512,512]{1,2,0:T(8,128)(4,1)}, pred[8,512,512]{1,2,0:T(8,128)(4,1)S(1)}, u32[]{:S(2)}) copy-start(pred[8,512,512]{1,2,0:T(8,128)(4,1)S(1)} %broadcast_and_fusion) | copy-start | bytes 6291460
  183.5 1.6 copy-start.6
  183.5 6.5 copy-start.15
  183.5 28.8 %copy-start.18 = (bf16[2,2,256]{2,1,0:T(2,128)(2,1)S(1)}, bf16[2,2,256]{2,1,0:T(2,128)(2,1)}, u32[]{:S(2)}) copy-start(bf16[2,2,256]{2,1,0:T(2,128)(2,1)} %param.18) | copy-start | bytes 6148
  183.6 344.9 %all-gather.29.cloned.1.call-start = ((), (), s32[]{:S(2)}) async-start(), calls=%async_computation.6 | async-start | bytes 9437184 | tf_op jit(solution)/shard_map/all_gather | solution.py:39
  186.6 390.6 %all-gather.31.cloned.1.call-start = ((), (), s32[]{:S(2)}) async-start(), calls=%async_computation.7 | async-start | bytes 9437184 | tf_op jit(solution)/shard_map/all_gather | solution.py:41
  189.9 718.7 %all-reduce.7.cloned.1.call-start = ((), (), s32[]{:S(2)}) async-start(), calls=%async_computation.1 | async-start | bytes 33554432 | tf_op jit(solution)/shard_map/psum | solution.py:54
  493.7 6.2 copy-start.1
  493.7 34.8 %copy-start.10 = (f32[1,1,2048]{2,1,0:T(1,128)S(1)}, f32[1,1,2048]{2,1,0:T(1,128)}, u32[]{:S(2)}) copy-start(f32[1,1,2048]{2,1,0:T(1,128)} %get-tuple-element.23) | copy-start | bytes 24580
  493.8 34.7 %copy-start.11 = (f32[1,1,2048]{2,1,0:T(1,128)S(1)}, f32[1,1,2048]{2,1,0:T(1,128)}, u32[]{:S(2)}) copy-start(f32[1,1,2048]{2,1,0:T(1,128)} %get-tuple-element.26) | copy-start | bytes 24580
  618.6 1.8 copy-start.9
  618.6 19.8 %copy-start.14 = (bf16[1,3,64]{2,0,1:T(2,128)(2,1)S(1)}, bf16[1,3,64]{2,0,1:T(2,128)(2,1)}, u32[]{:S(2)}) copy-start(bf16[1,3,64]{2,0,1:T(2,128)(2,1)} %get-tuple-element.36) | copy-start | bytes 1156
  618.6 290.0 %copy-start.7 = (f32[1,1,2048]{2,1,0:T(1,128)S(1)}, f32[1,1,2048]{2,1,0:T(1,128)}, u32[]{:S(2)}) copy-start(f32[1,1,2048]{2,1,0:T(1,128)} %get-tuple-element.32) | copy-start | bytes 24580
  618.7 333.3 %all-gather.33.cloned.1.call-start = ((), (), s32[]{:S(2)}) async-start(), calls=%async_computation.8 | async-start | bytes 7077888 | tf_op jit(solution)/shard_map/all_gather | solution.py:36
  619.5 425.0 %all-gather.35.cloned.1.call-start = ((), (), s32[]{:S(2)}) async-start(), calls=%async_computation.9 | async-start | bytes 2359296 | tf_op jit(solution)/shard_map/all_gather | solution.py:38
  620.3 729.7 %all-reduce.9.cloned.1.call-start = ((), (), s32[]{:S(2)}) async-start(), calls=%async_computation.2 | async-start | bytes 33554432 | tf_op jit(solution)/shard_map/psum | solution.py:48
  922.8 6.2 copy-start.2
  952.0 34.9 %copy-start.5 = (pred[8,512,512]{1,2,0:T(8,128)(4,1)S(1)}, pred[8,512,512]{1,2,0:T(8,128)(4,1)}, u32[]{:S(2)}) copy-start(pred[8,512,512]{1,2,0:T(8,128)(4,1)} %copy-done.4) | copy-start | bytes 6291460
  1059.4 1.6 copy-start.16
  1059.4 20.1 %copy-start.17 = (bf16[1,2,256]{2,1,0:T(2,128)(2,1)S(1)}, bf16[1,2,256]{2,1,0:T(2,128)(2,1)}, u32[]{:S(2)}) copy-start(bf16[1,2,256]{2,1,0:T(2,128)(2,1)} %get-tuple-element.34) | copy-start | bytes 3076
  1059.4 339.5 %all-gather.37.cloned.1.call-start = ((), (), s32[]{:S(2)}) async-start(), calls=%async_computation.10 | async-start | bytes 9437184 | tf_op jit(solution)/shard_map/all_gather | solution.py:39
  1060.1 387.7 %all-gather.39.cloned.1.call-start = ((), (), s32[]{:S(2)}) async-start(), calls=%async_computation.11 | async-start | bytes 9437184 | tf_op jit(solution)/shard_map/all_gather | solution.py:41
  1060.9 718.4 %all-reduce.11.cloned.1.call-start = ((), (), s32[]{:S(2)}) async-start(), calls=%async_computation.3 | async-start | bytes 33554432 | tf_op jit(solution)/shard_map/psum | solution.py:54
  1364.2 6.2 copy-start.3
  1364.2 34.7 %copy-start.12 = (f32[1,1,2048]{2,1,0:T(1,128)S(1)}, f32[1,1,2048]{2,1,0:T(1,128)}, u32[]{:S(2)}) copy-start(f32[1,1,2048]{2,1,0:T(1,128)} %get-tuple-element.19) | copy-start | bytes 24580
  1364.3 34.7 %copy-start.13 = (f32[1,1,2048]{2,1,0:T(1,128)S(1)}, f32[1,1,2048]{2,1,0:T(1,128)}, u32[]{:S(2)}) copy-start(f32[1,1,2048]{2,1,0:T(1,128)} %get-tuple-element.22) | copy-start | bytes 24580
  1489.3 290.0 %copy-start.8 = (f32[1,1,2048]{2,1,0:T(1,128)S(1)}, f32[1,1,2048]{2,1,0:T(1,128)}, u32[]{:S(2)}) copy-start(f32[1,1,2048]{2,1,0:T(1,128)} %get-tuple-element.27) | copy-start | bytes 24580
Sparse Core Ops, SparseCore 0:
  9.4 46.7 all-gather.24
  57.9 23.2 all-gather.26
  183.7 295.7 all-reduce.4
  481.0 47.4 all-gather.28
  530.0 47.1 all-gather.30
  618.8 289.7 all-reduce.6
  910.2 41.7 all-gather.32
  953.6 23.3 all-gather.34
  1059.6 290.4 all-reduce.8
  1351.5 47.4 all-gather.36
  1400.6 47.1 all-gather.38
  1489.5 289.7 all-reduce.10
where the time goes:
time: 1810 us
  waiting for transfers between devices  1110 us (61%)
  matrix products  382 us (21%)
  blocking collectives  168 us (9%)
  other arithmetic  93.3 us (5%)
  local copies, waits for them, and re-layouts  38.1 us (2%)
    psum x2, waiting for transfers between devices, per_device(): down_sum = lax.psum(down_part, 'tp')  537 us
    psum x2, waiting for transfers between devices, per_device(): attn_sum = lax.psum(attn_part, 'tp')  491 us
    dot_general x2, matrix products, per_device(): jnp.einsum('bsd,df->bsf', normed_mid, up_full, preferred_element_type=jnp...  84 us
    dot_general x2, matrix products, per_device(): jnp.einsum('bsf,fd->bsd', hidden_up, down_full, preferred_element_type=jn...  82.9 us
    dot_general x2, matrix products, per_device(): jnp.einsum('bsd,dkhe->bskhe', normed, qkv_full, preferred_element_type=jn...  70.3 us
    sub x2, matrix products, attend(): attn_probs = jax.nn.softmax(scores, axis=-1).astype(jnp.bfloat16)  64.6 us
    reduce_sum x4, other arithmetic, layer_norm(): row_mean = jnp.mean(as_f32, axis=-1, keepdims=True)  51.1 us
    dot_general x2, matrix products, attend(): jnp.einsum('bhqk,bkhe->bqhe', attn_probs, qkv_out[:, :, 2], preferred_ele...  50.5 us
  transfers between devices with their start and end apart: 12, of which 9 were waited for; matrix products, arithmetic and copies ran while one was open for 20% of the time, Pallas kernels for 0%

commit v1 on v0

v1 whole, which is shorter than its diff:
```python
import functools

import jax
import jax.numpy as jnp
from jax import lax
from jax.experimental import pallas as pl
from jax.experimental.pallas import tpu as pltpu
from jax.sharding import PartitionSpec as P


BOTH = ('tp', 'fsdp')
TILE = 512


def layer_norm(acts_in, ln_gain, ln_shift):
    as_f32 = acts_in.astype(jnp.float32)
    row_mean = jnp.mean(as_f32, axis=-1, keepdims=True)
    centered = as_f32 - row_mean
    row_var = jnp.mean(centered * centered, axis=-1, keepdims=True)
    return (centered * lax.rsqrt(row_var + 1e-5) * ln_gain + ln_shift).astype(jnp.bfloat16)


def attn_kernel(head_dim, heads, lens_ref, q_ref, k_ref, v_ref, o_ref):
    seq_len = q_ref.shape[1]
    half = seq_len // 2
    length = lens_ref[pl.program_id(0)]
    last = jnp.minimum(lax.broadcasted_iota(jnp.int32, (1, seq_len), 1), length - 1)
    key = lax.broadcasted_iota(jnp.int32, (half, seq_len), 0)
    early_ok = key <= last
    late_ok = key[:, :half] + half <= last[:, half:]
    keys_by_queries = (((1,), (1,)), ((), ()))
    over_keys = (((0,), (0,)), ((), ()))
    columns = [slice(h * head_dim, (h + 1) * head_dim) for h in range(heads)]
    scores = []
    for c in columns:
        q = q_ref[0, :, c] * jnp.bfloat16(head_dim ** -0.5)
        early = lax.dot_general(k_ref[0, :half, c], q, keys_by_queries, preferred_element_type=jnp.float32)
        late = lax.dot_general(k_ref[0, half:, c], q[half:], keys_by_queries, preferred_element_type=jnp.float32)
        scores.append((early, late))
    outs = []
    for c, (early, late) in zip(columns, scores):
        early = jnp.where(early_ok, early, -1e30)
        late = jnp.where(late_ok, late, -1e30)
        top = jnp.max(early, axis=0, keepdims=True)
        late_top = jnp.maximum(top[:, half:], jnp.max(late, axis=0, keepdims=True))
        early = jnp.exp(early - jnp.concatenate([top[:, :half], late_top], axis=1))
        late = jnp.exp(late - late_top)
        total = jnp.sum(early, axis=0, keepdims=True)
        late_total = total[:, half:] + jnp.sum(late, axis=0, keepdims=True)
        scale = 1.0 / jnp.concatenate([total[:, :half], late_total], axis=1)
        early = (early * scale).astype(jnp.bfloat16)
        late = (late * scale[:, half:]).astype(jnp.bfloat16)
        v = v_ref[0, :, c]
        first = lax.dot_general(v[:half], early[:, :half], over_keys, preferred_element_type=jnp.float32)
        second = lax.dot_general(v, jnp.concatenate([early[:, half:], late], axis=0), over_keys, preferred_element_type=jnp.float32)
        outs.append(jnp.concatenate([first, second], axis=1))
    o_ref[0] = jnp.concatenate(outs, axis=0).T.astype(jnp.bfloat16)


def attend(qkv, lens, share, head_dim):
    seqs, seq_len, total = qkv.shape
    width = total // 3
    block = 256
    per = share // block
    spec = lambda part: pl.BlockSpec((1, seq_len, block), lambda s, g, h, lens: (s, 0, (g * 3 + part) * per + h))
    return pl.pallas_call(
        functools.partial(attn_kernel, head_dim, block // head_dim),
        out_shape=jax.ShapeDtypeStruct((seqs, seq_len, width), jnp.bfloat16),
        grid_spec=pltpu.PrefetchScalarGridSpec(
            num_scalar_prefetch=1,
            grid=(seqs, width // share, per),
            in_specs=[spec(0), spec(1), spec(2)],
            out_specs=pl.BlockSpec((1, seq_len, block), lambda s, g, h, lens: (s, 0, g * per + h)),
        ),
        compiler_params=pltpu.CompilerParams(vmem_limit_bytes=40 * 1024 * 1024),
        cost_estimate=pl.CostEstimate(flops=16 * seqs * seq_len * seq_len * width, bytes_accessed=8 * seqs * seq_len * width, transcendentals=seqs * seq_len * seq_len * width // head_dim),
    )(lens, qkv, qkv, qkv)


def mm_kernel(relu, steps, x_ref, w_ref, b_ref, *refs):
    resid_ref = refs[0] if len(refs) == 3 else None
    o_ref, acc_ref = refs[-2:]
    k = pl.program_id(1)
    rows = x_ref.shape[0]
    w = w_ref[...].reshape(-1, w_ref.shape[2])
    half = min(512, rows)

    def start(r):
        base = jnp.broadcast_to(b_ref[...], (half, w.shape[1]))
        return base if resid_ref is None else base + resid_ref[r, :].astype(jnp.float32)

    for r0 in range(0, rows, half):
        r = pl.ds(r0, half)
        if steps == 1:
            total = jnp.dot(x_ref[r, :], w, preferred_element_type=jnp.float32) + start(r)
            o_ref[r, :] = (jnp.maximum(total, 0.0) if relu else total).astype(o_ref.dtype)
            continue

        @pl.when(k == 0)
        def _():
            acc_ref[r, :] = start(r)

        acc_ref[r, :] += jnp.dot(x_ref[r, :], w, preferred_element_type=jnp.float32)

        @pl.when(k == steps - 1)
        def _():
            o_ref[r, :] = acc_ref[r, :].astype(o_ref.dtype)


def matmul(x, w, bias, n, steps, w_block, w_index, resid=None, relu=False, first=0):
    rows, depth = x.shape
    tile = w_block[2]
    in_specs = [
        pl.BlockSpec((rows, depth // steps), lambda j, k: (0, k)),
        pl.BlockSpec(w_block, w_index),
        pl.BlockSpec((1, tile), lambda j, k: (0, first + j)),
    ]
    args = [x, w, bias.reshape(1, -1)]
    if resid is not None:
        in_specs.append(pl.BlockSpec((rows, tile), lambda j, k: (0, first + j)))
        args.append(resid)
    return pl.pallas_call(
        functools.partial(mm_kernel, relu, steps),
        out_shape=jax.ShapeDtypeStruct((rows, n), jnp.bfloat16),
        grid=(n // tile, steps),
        in_specs=in_specs,
        out_specs=pl.BlockSpec((rows, tile), lambda j, k: (0, j)),
        scratch_shapes=[pltpu.VMEM((rows, tile) if steps > 1 else (8, 128), jnp.float32)],
        compiler_params=pltpu.CompilerParams(vmem_limit_bytes=48 * 1024 * 1024),
        cost_estimate=pl.CostEstimate(flops=2 * rows * depth * n, bytes_accessed=2 * (depth * n + rows * (depth + n)), transcendentals=0),
    )(*args)


def place(out, x, step, column, size, total, width):
    rows, tile = x.shape
    piece = rows // 4

    def kernel(x_ref, *refs):
        o_ref, sem = refs[-2:]
        owner = lax.rem(lax.axis_index('tp') + step + size, size)
        row = pl.multiple_of(owner * rows + pl.program_id(0) * piece, piece)
        copy = pltpu.make_async_copy(x_ref, o_ref.at[pl.ds(row, piece), pl.ds(column * tile, tile)], sem)
        copy.start()
        copy.wait()

    whole = pl.BlockSpec(memory_space=pltpu.HBM)
    return pl.pallas_call(
        kernel,
        out_shape=jax.ShapeDtypeStruct((total, width), x.dtype),
        grid=(rows // piece,),
        in_specs=[pl.BlockSpec((piece, tile), lambda i: (i, 0))] + ([] if out is None else [whole]),
        out_specs=whole,
        scratch_shapes=[pltpu.SemaphoreType.DMA],
        input_output_aliases={} if out is None else {1: 0},
        compiler_params=pltpu.CompilerParams(vmem_limit_bytes=8 * 1024 * 1024),
        cost_estimate=pl.CostEstimate(flops=x.size, bytes_accessed=4 * x.size, transcendentals=0),
    )(*([x] if out is None else [x, out]))


def solution(mesh):
    rows_spec = P(('dp', 'fsdp'), None, None)
    in_specs = (rows_spec, P(('dp', 'fsdp')), P(None, 'fsdp', None, 'tp', None), P(None, None, ('tp', 'fsdp')), P(None, ('tp', 'fsdp'), None), P(None, 'fsdp', 'tp'), P(None, ('tp', 'fsdp')), P(None, ('tp', 'fsdp'), None), P(None, None, 'fsdp'), P(None, None, 'fsdp'))
    tp = mesh.shape['tp']
    fs = mesh.shape['fsdp']

    def per_device(hidden, seq_lens, w_qkv, b_qkv, w_proj, w_up, b_up, w_down, b_resid, ln_params):
        n_layers, rows, _, local_heads, head_dim = w_qkv.shape
        seq_len, d_model = hidden.shape[1:]
        share = local_heads * head_dim
        ff = w_up.shape[2]
        proj_rows = w_proj.shape[1]
        my_seqs = hidden.shape[0] // tp
        me = lax.axis_index('tp')

        def gather(x):
            return lax.all_gather(x, BOTH, axis=0, tiled=False)

        qkv_loc = [w_qkv[l].reshape(rows, 3 * share) for l in range(n_layers)]
        groups = rows // proj_rows
        proj_loc = [w_proj[l].reshape(proj_rows, groups, -1).transpose(1, 0, 2).reshape(rows, -1) for l in range(n_layers)]
        assert proj_loc[0].shape[1] == TILE and n_layers == 2
        g1 = gather(qkv_loc[0])
        g2 = gather(jnp.concatenate([w_up[0], w_down[0], qkv_loc[1], proj_loc[0]], axis=1))
        g3 = gather(jnp.concatenate([w_up[1], proj_loc[1]], axis=1))
        g4 = gather(w_down[1])
        wide_tiles = d_model // TILE
        ff_tiles = ff // TILE
        qkv_at = [(g1, 0), (g2, ff_tiles + wide_tiles)]
        proj_at = [(g2, ff_tiles + wide_tiles + 3 * share // TILE), (g3, ff_tiles)]
        up_at = [(g2, 0), (g3, 0)]
        down_at = [(g2, ff_tiles), (g4, 0)]

        small = gather(jnp.concatenate([b_qkv.reshape(n_layers, -1), b_up], axis=1)).astype(jnp.float32)
        small = small.reshape(tp, fs, n_layers, -1)
        piece = share // fs
        qkv_bias = small[..., :3 * piece].reshape(tp, fs, n_layers, 3, piece).transpose(2, 0, 3, 1, 4).reshape(n_layers, -1)
        up_bias = small[..., 3 * piece:].transpose(2, 0, 1, 3).reshape(n_layers, -1)
        wide = lax.all_gather(jnp.concatenate([ln_params, b_resid.astype(jnp.float32)], axis=1), 'fsdp', axis=2, tiled=True)

        current = lax.dynamic_slice_in_dim(hidden, me * my_seqs, my_seqs, 0).reshape(my_seqs * seq_len, d_model)
        lens = lax.dynamic_slice_in_dim(seq_lens, me * my_seqs, my_seqs, 0)

        per = 3 * share // TILE
        for l in range(n_layers):
            normed = layer_norm(current, wide[l, 0], wide[l, 1])
            w, c0 = qkv_at[l]
            qkv = matmul(normed, w, qkv_bias[l], tp * 3 * share, 1, (fs, rows, TILE), lambda j, k, c0=c0: (j // per, 0, c0 + j % per))
            context = attend(qkv.reshape(my_seqs, seq_len, -1), lens, share, head_dim)
            w, c0 = proj_at[l]
            mid = matmul(context.reshape(my_seqs * seq_len, -1), w, wide[l, 4], d_model, 1, (tp * fs, proj_rows, TILE), lambda j, k, c0=c0: (0, j, c0), resid=current)
            normed_mid = layer_norm(mid, wide[l, 2], wide[l, 3])
            w, c0 = up_at[l]
            u = matmul(normed_mid, w, up_bias[l], tp * ff, 1, (fs, rows, TILE), lambda j, k, c0=c0: (j // ff_tiles, 0, c0 + j % ff_tiles), relu=True)
            w, c0 = down_at[l]
            down = lambda first, n: matmul(u, w, wide[l, 5], n, tp, (fs, rows, TILE), lambda j, k: (k, 0, c0 + first + j), resid=mid, first=first)
            if l + 1 < n_layers:
                current = down(0, d_model)
        plus = [(i, (i + 1) % tp) for i in range(tp)]
        minus = [(i, (i - 1) % tp) for i in range(tp)]
        blocks = []
        for j in range(wide_tiles):
            own = down(j, TILE)
            right = lax.ppermute(own, 'tp', plus)
            left = lax.ppermute(own, 'tp', minus)
            blocks += [(0, j, own), (-1, j, right), (1, j, left)]
        for j in range(wide_tiles):
            here, perm = (blocks[3 * j + 1], plus) if j < wide_tiles // 2 else (blocks[3 * j + 2], minus)
            blocks.append((2, j, lax.ppermute(here[2], 'tp', perm)))
        out = None
        for step, j, x in blocks:
            out = place(out, x, step, j, tp, tp * my_seqs * seq_len, d_model)
        return out.reshape(hidden.shape)

    return jax.shard_map(per_device, mesh=mesh, in_specs=in_specs, out_specs=rows_spec, check_vma=False)
```

time: 1810 us -> 802 us (0.44)
  waiting for transfers between devices: 1110 us -> 284 us
  matrix products: 382 us -> 0 us
  Pallas kernels: 0 us -> 378 us
  blocking collectives: 168 us -> 57.6 us
  other arithmetic: 93.3 us -> 27.8 us
  local copies, waits for them, and re-layouts: 38.1 us -> 18.8 us
    psum x4 -> x0, waiting for transfers between devices: 1030 us -> none  [the longest x2 537 us: per_device(): down_sum = lax.psum(down_part, 'tp')]
    pallas_call x0 -> x29, Pallas kernels: none -> 378 us  [the longest x11 276 us: matmul(): pl.pallas_call(functools.partial(mm_kernel, relu, steps), out_shape=jax.S...]
    dot_general x10 -> x0, matrix products: 318 us -> none  [the longest x2 84 us: per_device(): jnp.einsum('bsd,df->bsf', normed_mid, up_full, preferred_element_type=jnp...]
    all_gather x8 -> x4, waiting for transfers between devices: 77.2 us -> 240 us  [gather(): return lax.all_gather(x, BOTH, axis=0, tiled=False)]
    all_gather x8 -> x2, blocking collectives: 168 us -> 57.6 us  [the longest x1 32.5 us: gather(): return lax.all_gather(x, BOTH, axis=0, tiled=False)]
    sub x2 -> x0, matrix products: 64.6 us -> none  [attend(): attn_probs = jax.nn.softmax(scores, axis=-1).astype(jnp.bfloat16)]
    reduce_sum x4, other arithmetic: 51.1 us -> 6.76 us  [layer_norm(): row_mean = jnp.mean(as_f32, axis=-1, keepdims=True)]
    ppermute x0 -> x12, waiting for transfers between devices: none -> 43.1 us  [the longest x4 19 us: per_device(): right = lax.ppermute(own, 'tp', plus)]
  transfers between devices with their start and end apart: 12 -> 16, of which waited for: 9 -> 6; matrix products, arithmetic and copies ran while one was open for 20% -> 4% of each run, Pallas kernels for 0% -> 45%
where the time goes in v1:
time: 802 us; the launch traced here: 796 us
  Pallas kernels  378 us (47%)
  waiting for transfers between devices  284 us (35%)
  blocking collectives  57.6 us (7%)
  other arithmetic  27.8 us (3%)
  local copies, waits for them, and re-layouts  18.8 us (2%)
  starting transfers between devices  16.2 us (2%)
  between operations  14.1 us (2%)
    pallas_call x11, Pallas kernels, matmul(): pl.pallas_call(functools.partial(mm_kernel, relu, steps), out_shape=jax.S...  276 us
    all_gather x4, waiting for transfers between devices, gather(): return lax.all_gather(x, BOTH, axis=0, tiled=False)  240 us
    pallas_call x2, Pallas kernels, attend(): pl.pallas_call(functools.partial(attn_kernel, head_dim, block // head_dim...  56.2 us
    pallas_call x16, Pallas kernels, place(): pl.pallas_call(kernel, out_shape=jax.ShapeDtypeStruct((total, width), x.d...  45.6 us
    all_gather x1, blocking collectives, gather(): return lax.all_gather(x, BOTH, axis=0, tiled=False)  32.5 us
    all_gather x1, blocking collectives, per_device(): lax.all_gather(jnp.concatenate([ln_params, b_resid.astype(jnp.float32)],...  25.1 us
    ppermute x4, waiting for transfers between devices, per_device(): right = lax.ppermute(own, 'tp', plus)  19 us
    ppermute x4, waiting for transfers between devices, per_device(): left = lax.ppermute(own, 'tp', minus)  18.8 us
  transfers between devices with their start and end apart: 16, of which 6 were waited for; matrix products, arithmetic and copies ran while one was open for 4% of the time, Pallas kernels for 45%

profile of v1, /device:TPU:97, one launch (start us, length us, event | category | flops | bytes accessed | tf_op | source)
XLA Modules:
  0.0 796.4 jit_solution(16917126010559267695)
XLA Ops:
  6.6 1.5 fusion.22
  8.0 1.2 copy.41
  9.6 1.1 fusion.23
  10.9 2.8 fusion.21
  13.7 1.7 slice_bitcast_fusion
  15.4 1.8 pad_maximum_fusion
  17.6 1.2 pad_maximum_fusion.1
  19.7 32.5 %all-gather.3 = bf16[32,2,448]{2,1,0:T(2,128)(2,1)S(1)} all-gather(bf16[1,2,448]{2,1,0:T(2,128)(2,1)S(1)} %maximum_bitcast_fusion), channel_id=2, replica_groups=mesh['dp'=1,'tp'=4,'fsdp'=8] {'tp','fsdp'}, dimensions={0}, use_global_device_ids=true | all-gather | bytes 59136 | tf_op jit(solution)/shard_map/all_gather | solution.py:176
  52.4 4.9 convert_reduce_fusion.3
  57.3 3.5 fusion.19
  61.4 25.1 %all_gather.27 = f32[2,6,2048]{2,1,0:T(8,128)S(1)} all-gather(f32[2,6,256]{2,1,0:T(8,128)S(1)} %pad_maximum_fusion.2), channel_id=1, replica_groups=mesh['dp'=1,'tp'=4,'fsdp'=8] {'fsdp'}, dimensions={2}, use_global_device_ids=true | all-gather | bytes 110592 | tf_op jit(solution)/shard_map/all_gather | solution.py:198
  86.5 0.7 slice_bitcast_fusion.5
  87.2 5.1 add_convert_fusion.x_ref
  92.3 8.4 %all-gather.9.cloned.1.call-done.w_ref = bf16[32,256,1536]{2,1,0:T(8,128)(2,1)} async-done(((bf16[1,256,1536]{2,1,0:T(8,128)(2,1)}), bf16[32,256,1536]{2,1,0:T(8,128)(2,1)}) %all-gather.9.cloned.1.call-update) | async-done | bytes 25165840 | tf_op jit(solution)/shard_map/all_gather | solution.py:176
  100.8 2.2 copy-done.6
  102.9 31.0 %shard_map.100 = bf16[1024,6144]{1,0:T(8,128)(2,1)} custom-call(bf16[1024,2048]{1,0:T(8,128)(2,1)S(1)} %copy-done.6, bf16[32,256,1536]{2,1,0:T(8,128)(2,1)} %all-gather.9.cloned.1.call-done.w_ref, f32[1,6144]{1,0:T(1,128)S(1)} %slice.98.b_ref), custom_call_target="tpu_custom_call" | custom-call | flops 25769803776 | bytes 41943040 | tf_op jit(solution)/shard_map/pallas_call | solution.py:122
  133.9 28.1 %shard_map.101 = bf16[2,512,2048]{2,1,0:T(8,128)(2,1)S(1)} custom-call(s32[2]{0:T(128)S(1)} %dynamic_slice.6.lens_ref, bf16[2,512,6144]{2,1,0:T(8,128)(2,1)} %bitcast.96, bf16[2,512,6144]{2,1,0:T(8,128)(2,1)} %bitcast.97, bf16[2,512,6144]{2,1,0:T(8,128)(2,1)} %bitcast.98), custom_call_target="tpu_custom_call" | custom-call | flops 17179869184 | bytes 16777216 | tf_op jit(solution)/shard_map/pallas_call | solution.py:66
  162.1 2.0 copy-done.4
  164.1 221.2 %all-gather.13.cloned.1.call-done = bf16[8192,6144]{1,0:T(8,128)(2,1)} async-done(((bf16[256,6144]{1,0:T(8,128)(2,1)}), bf16[8192,6144]{1,0:T(8,128)(2,1)}) %all-gather.13.cloned.1.call-update) | async-done | bytes 100663312 | tf_op jit(solution)/shard_map/all_gather | solution.py:176
  385.3 12.9 %shard_map.102.refs_0_ = bf16[1024,2048]{1,0:T(8,128)(2,1)S(1)} custom-call(bf16[1024,2048]{1,0:T(8,128)(2,1)} %bitcast.69, bf16[32,256,6144]{2,1,0:T(8,128)(2,1)} %bitcast.14.w_ref, f32[1,2048]{1,0:T(1,128)S(1)} %get-tuple-element.24.b_ref, bf16[1024,2048]{1,0:T(8,128)(2,1)} %bitcast.refs_0_), custom_call_target="tpu_custom_call" | custom-call | flops 8589934592 | bytes 16777216 | tf_op jit(solution)/shard_map/pallas_call | solution.py:122
  398.8 1.2 fusion.14
  400.1 1.9 fusion.17.x_ref
  402.0 40.6 %shard_map.103.x_ref = bf16[1024,8192]{1,0:T(8,128)(2,1)} custom-call(bf16[1024,2048]{1,0:T(8,128)(2,1)S(1)} %fusion.17.x_ref, bf16[32,256,6144]{2,1,0:T(8,128)(2,1)} %bitcast.14.w_ref, f32[1,8192]{1,0:T(1,128)S(1)} %bitcast.72), custom_call_target="tpu_custom_call" | custom-call | flops 34359738368 | bytes 54525952 | tf_op jit(solution)/shard_map/pallas_call | solution.py:122
  442.6 52.0 %shard_map.104.refs_0_ = bf16[1024,2048]{1,0:T(8,128)(2,1)S(1)} custom-call(bf16[1024,8192]{1,0:T(8,128)(2,1)} %shard_map.103.x_ref, bf16[32,256,6144]{2,1,0:T(8,128)(2,1)} %bitcast.14.w_ref, f32[1,2048]{1,0:T(1,128)S(1)} %get-tuple-element.21.b_ref, bf16[1024,2048]{1,0:T(8,128)(2,1)} %copy-done.2), custom_call_target="tpu_custom_call" | custom-call | flops 34359738368 | bytes 54525952 | tf_op jit(solution)/shard_map/pallas_call | solution.py:122
  495.2 1.2 fusion.10
  496.5 1.8 fusion.13.x_ref
  498.3 30.9 %shard_map.105 = bf16[1024,6144]{1,0:T(8,128)(2,1)} custom-call(bf16[1024,2048]{1,0:T(8,128)(2,1)S(1)} %fusion.13.x_ref, bf16[32,256,6144]{2,1,0:T(8,128)(2,1)} %bitcast.14.w_ref, f32[1,6144]{1,0:T(1,128)S(1)} %slice.113.b_ref), custom_call_target="tpu_custom_call" | custom-call | flops 25769803776 | bytes 41943040 | tf_op jit(solution)/shard_map/pallas_call | solution.py:122
  529.2 28.1 %shard_map.106 = bf16[2,512,2048]{2,1,0:T(8,128)(2,1)S(1)} custom-call(s32[2]{0:T(128)S(1)} %dynamic_slice.6.lens_ref, bf16[2,512,6144]{2,1,0:T(8,128)(2,1)} %bitcast.75, bf16[2,512,6144]{2,1,0:T(8,128)(2,1)} %bitcast.76, bf16[2,512,6144]{2,1,0:T(8,128)(2,1)} %bitcast.77), custom_call_target="tpu_custom_call" | custom-call | flops 17179869184 | bytes 16777216 | tf_op jit(solution)/shard_map/pallas_call | solution.py:66
  557.4 2.0 copy-done.5
  559.4 12.9 %shard_map.107.refs_0_ = bf16[1024,2048]{1,0:T(8,128)(2,1)S(1)} custom-call(bf16[1024,2048]{1,0:T(8,128)(2,1)} %bitcast.70, bf16[32,256,2560]{2,1,0:T(8,128)(2,1)} %bitcast.73, f32[1,2048]{1,0:T(1,128)S(1)} %get-tuple-element.18.b_ref, bf16[1024,2048]{1,0:T(8,128)(2,1)} %copy-done.3), custom_call_target="tpu_custom_call" | custom-call | flops 8589934592 | bytes 16777216 | tf_op jit(solution)/shard_map/pallas_call | solution.py:122
  572.9 1.2 fusion.6
  574.2 1.9 fusion.9.x_ref
  576.1 40.4 %shard_map.108.x_ref = bf16[1024,8192]{1,0:T(8,128)(2,1)} custom-call(bf16[1024,2048]{1,0:T(8,128)(2,1)S(1)} %fusion.9.x_ref, bf16[32,256,2560]{2,1,0:T(8,128)(2,1)} %bitcast.74, f32[1,8192]{1,0:T(1,128)S(1)} %bitcast.71), custom_call_target="tpu_custom_call" | custom-call | flops 34359738368 | bytes 54525952 | tf_op jit(solution)/shard_map/pallas_call | solution.py:122
  616.4 10.2 %all-gather.11.cloned.1.call-done.w_ref = bf16[32,256,2048]{2,1,0:T(8,128)(2,1)} async-done(((bf16[1,256,2048]{2,1,0:T(8,128)(2,1)}), bf16[32,256,2048]{2,1,0:T(8,128)(2,1)}) %all-gather.11.cloned.1.call-update) | async-done | bytes 33554448 | tf_op jit(solution)/shard_map/all_gather | solution.py:176
  626.6 2.2 copy-done.1
  628.8 14.1 %shard_map.112.x_ref = bf16[1024,512]{1,0:T(8,128)(2,1)S(1)} custom-call(bf16[1024,8192]{1,0:T(8,128)(2,1)} %shard_map.108.x_ref, bf16[32,256,2048]{2,1,0:T(8,128)(2,1)} %all-gather.11.cloned.1.call-done.w_ref, f32[1,2048]{1,0:T(1,128)S(1)} %get-tuple-element.15.b_ref, bf16[1024,2048]{1,0:T(8,128)(2,1)S(1)} %copy-done.1), custom_call_target="tpu_custom_call" | custom-call | flops 8589934592 | bytes 26214400 | tf_op jit(solution)/shard_map/pallas_call | solution.py:122
  643.4 2.3 collective-permute-start.11
  645.7 13.9 %shard_map.111.x_ref = bf16[1024,512]{1,0:T(8,128)(2,1)S(1)} custom-call(bf16[1024,8192]{1,0:T(8,128)(2,1)} %shard_map.108.x_ref, bf16[32,256,2048]{2,1,0:T(8,128)(2,1)} %all-gather.11.cloned.1.call-done.w_ref, f32[1,2048]{1,0:T(1,128)S(1)} %get-tuple-element.15.b_ref, bf16[1024,2048]{1,0:T(8,128)(2,1)S(1)} %copy-done.1), custom_call_target="tpu_custom_call" | custom-call | flops 8589934592 | bytes 26214400 | tf_op jit(solution)/shard_map/pallas_call | solution.py:122
  659.7 2.6 collective-permute-start.10
  662.4 13.9 %shard_map.110.x_ref = bf16[1024,512]{1,0:T(8,128)(2,1)S(1)} custom-call(bf16[1024,8192]{1,0:T(8,128)(2,1)} %shard_map.108.x_ref, bf16[32,256,2048]{2,1,0:T(8,128)(2,1)} %all-gather.11.cloned.1.call-done.w_ref, f32[1,2048]{1,0:T(1,128)S(1)} %get-tuple-element.15.b_ref, bf16[1024,2048]{1,0:T(8,128)(2,1)S(1)} %copy-done.1), custom_call_target="tpu_custom_call" | custom-call | flops 8589934592 | bytes 26214400 | tf_op jit(solution)/shard_map/pallas_call | solution.py:122
  676.4 2.6 collective-permute-start.2
  679.1 13.9 %shard_map.109.x_ref = bf16[1024,512]{1,0:T(8,128)(2,1)S(1)} custom-call(bf16[1024,8192]{1,0:T(8,128)(2,1)} %shard_map.108.x_ref, bf16[32,256,2048]{2,1,0:T(8,128)(2,1)} %all-gather.11.cloned.1.call-done.w_ref, f32[1,2048]{1,0:T(1,128)S(1)} %get-tuple-element.15.b_ref, bf16[1024,2048]{1,0:T(8,128)(2,1)S(1)} %copy-done.1), custom_call_target="tpu_custom_call" | custom-call | flops 8589934592 | bytes 26214400 | tf_op jit(solution)/shard_map/pallas_call | solution.py:122
  693.1 1.4 collective-permute-start.8
  694.7 19.0 %collective-permute-done.9.x_ref = bf16[1024,512]{1,0:T(8,128)(2,1)S(1)} collective-permute-done((bf16[1024,512]{1,0:T(8,128)(2,1)S(1)}, bf16[1024,512]{1,0:T(8,128)(2,1)S(1)}, u32[]{:S(2)}, u32[]{:S(2)}) %collective-permute-start.9) | collective-permute-done | bytes 1048608 | tf_op jit(solution)/shard_map/ppermute | solution.py:223
  713.6 2.7 collective-permute-start.3
  716.3 18.8 %collective-permute-done.x_ref = bf16[1024,512]{1,0:T(8,128)(2,1)S(1)} collective-permute-done((bf16[1024,512]{1,0:T(8,128)(2,1)S(1)}, bf16[1024,512]{1,0:T(8,128)(2,1)S(1)}, u32[]{:S(2)}, u32[]{:S(2)}) %collective-permute-start) | collective-permute-done | bytes 1048608 | tf_op jit(solution)/shard_map/ppermute | solution.py:224
  735.1 3.4 collective-permute-start.1
  738.5 2.8 shard_map.113.refs_0_
  741.3 2.9 shard_map.114.refs_0_
  744.2 2.9 shard_map.115.refs_0_
  747.0 2.9 shard_map.116.refs_0_
  749.9 2.9 shard_map.117.refs_0_
  752.8 2.9 shard_map.118.refs_0_
  755.6 2.9 shard_map.119.refs_0_
  758.5 2.9 shard_map.120.refs_0_
  761.4 2.9 shard_map.121.refs_0_
  764.2 2.9 shard_map.122.refs_0_
  767.1 2.9 shard_map.123.refs_0_
  770.0 2.9 shard_map.124.refs_0_
  772.8 2.9 shard_map.125.refs_0_
  775.7 5.3 collective-permute-done.5.x_ref
  781.0 2.8 shard_map.126.refs_0_
  783.9 2.9 shard_map.127.refs_0_
  786.7 2.9 shard_map.128
  (89 shorter events, 5.4 us)
Async XLA Ops:
  6.5 94.2 %all-gather.9.cloned.1.call-start = ((), (), s32[]{:S(2)}) async-start(), calls=%async_computation | async-start | bytes 25952256 | tf_op jit(solution)/shard_map/all_gather | solution.py:176
  9.3 376.1 %all-gather.13.cloned.1.call-start = ((), (), s32[]{:S(2)}) async-start(), calls=%async_computation.2 | async-start | bytes 103809024 | tf_op jit(solution)/shard_map/all_gather | solution.py:176
  15.4 4.1 copy-start.13
  15.4 4.2 copy-start.14
  17.3 542.1 %all-gather.15.cloned.1.call-start = ((), (), s32[]{:S(2)}) async-start(), calls=%async_computation.3 | async-start | bytes 43253760 | tf_op jit(solution)/shard_map/all_gather | solution.py:176
  17.6 43.2 %copy-start.12 = (bf16[2,2,256]{2,1,0:T(2,128)(2,1)S(1)}, bf16[2,2,256]{2,1,0:T(2,128)(2,1)}, u32[]{:S(2)}) copy-start(bf16[2,2,256]{2,1,0:T(2,128)(2,1)} %param.18) | copy-start | bytes 6148
  18.8 42.3 %copy-start.15 = (s32[8]{0:T(128)S(1)}, s32[8]{0:T(128)}, u32[]{:S(2)}) copy-start(s32[8]{0:T(128)} %param.11) | copy-start | bytes 100
  18.8 42.6 %copy-start.11 = (f32[2,4,256]{2,1,0:T(4,128)S(1)}, f32[2,4,256]{2,1,0:T(4,128)}, u32[]{:S(2)}) copy-start(f32[2,4,256]{2,1,0:T(4,128)} %param.19) | copy-start | bytes 24580
  18.9 607.7 %all-gather.11.cloned.1.call-start = ((), (), s32[]{:S(2)}) async-start(), calls=%async_computation.1 | async-start | bytes 34603008 | tf_op jit(solution)/shard_map/all_gather | solution.py:176
  100.7 2.2 copy-start.6
  162.1 2.0 copy-start.4
  398.2 3.8 copy-start.2
  494.5 1.9 copy-start.3
  494.6 1.9 copy-start.9
  494.6 1.9 copy-start.10
  557.4 2.0 copy-start.5
  572.2 3.8 copy-start
  572.3 1.9 copy-start.7
  572.3 1.9 copy-start.8
  626.6 2.2 copy-start.1
  642.9 33.5 %collective-permute-start.6 = (bf16[1024,512]{1,0:T(8,128)(2,1)S(1)}, bf16[1024,512]{1,0:T(8,128)(2,1)S(1)}, u32[]{:S(2)}, u32[]{:S(2)}) collective-permute-start(bf16[1024,512]{1,0:T(8,128)(2,1)S(1)} %shard_map.112.x_ref), channel_id=1, source_target_pairs={{0,8},{8,16},{16,24},{24,0},{1,9},{9,17},{17,25},{25,1},{2,10},{10... | collective-permute-start | bytes 3145736 | tf_op jit(solution)/shard_map/ppermute | solution.py:223
  643.4 49.6 %collective-permute-start.11 = (bf16[1024,512]{1,0:T(8,128)(2,1)S(1)}, bf16[1024,512]{1,0:T(8,128)(2,1)S(1)}, u32[]{:S(2)}, u32[]{:S(2)}) collective-permute-start(bf16[1024,512]{1,0:T(8,128)(2,1)S(1)} %shard_map.112.x_ref), channel_id=1, source_target_pairs={{0,24},{8,0},{16,8},{24,16},{1,25},{9,1},{17,9},{25,17},{2,26},{10... | collective-permute-start | bytes 3145736 | tf_op jit(solution)/shard_map/ppermute | solution.py:224
  659.6 33.5 %collective-permute-start.4 = (bf16[1024,512]{1,0:T(8,128)(2,1)S(1)}, bf16[1024,512]{1,0:T(8,128)(2,1)S(1)}, u32[]{:S(2)}, u32[]{:S(2)}) collective-permute-start(bf16[1024,512]{1,0:T(8,128)(2,1)S(1)} %shard_map.111.x_ref), channel_id=1, source_target_pairs={{0,8},{8,16},{16,24},{24,0},{1,9},{9,17},{17,25},{25,1},{2,10},{10... | collective-permute-start | bytes 3145736 | tf_op jit(solution)/shard_map/ppermute | solution.py:223
  659.7 34.9 %collective-permute-start.10 = (bf16[1024,512]{1,0:T(8,128)(2,1)S(1)}, bf16[1024,512]{1,0:T(8,128)(2,1)S(1)}, u32[]{:S(2)}, u32[]{:S(2)}) collective-permute-start(bf16[1024,512]{1,0:T(8,128)(2,1)S(1)} %shard_map.111.x_ref), channel_id=1, source_target_pairs={{0,24},{8,0},{16,8},{24,16},{1,25},{9,1},{17,9},{25,17},{2,26},{10... | collective-permute-start | bytes 3145736 | tf_op jit(solution)/shard_map/ppermute | solution.py:224
  676.3 37.3 %collective-permute-start.9 = (bf16[1024,512]{1,0:T(8,128)(2,1)S(1)}, bf16[1024,512]{1,0:T(8,128)(2,1)S(1)}, u32[]{:S(2)}, u32[]{:S(2)}) collective-permute-start(bf16[1024,512]{1,0:T(8,128)(2,1)S(1)} %shard_map.110.x_ref), channel_id=1, source_target_pairs={{0,8},{8,16},{16,24},{24,0},{1,9},{9,17},{17,25},{25,1},{2,10},{10... | collective-permute-start | bytes 3145736 | tf_op jit(solution)/shard_map/ppermute | solution.py:223
  676.4 37.2 %collective-permute-start.2 = (bf16[1024,512]{1,0:T(8,128)(2,1)S(1)}, bf16[1024,512]{1,0:T(8,128)(2,1)S(1)}, u32[]{:S(2)}, u32[]{:S(2)}) collective-permute-start(bf16[1024,512]{1,0:T(8,128)(2,1)S(1)} %shard_map.110.x_ref), channel_id=1, source_target_pairs={{0,24},{8,0},{16,8},{24,16},{1,25},{9,1},{17,9},{25,17},{2,26},{10... | collective-permute-start | bytes 3145736 | tf_op jit(solution)/shard_map/ppermute | solution.py:224
  693.0 42.1 %collective-permute-start = (bf16[1024,512]{1,0:T(8,128)(2,1)S(1)}, bf16[1024,512]{1,0:T(8,128)(2,1)S(1)}, u32[]{:S(2)}, u32[]{:S(2)}) collective-permute-start(bf16[1024,512]{1,0:T(8,128)(2,1)S(1)} %shard_map.109.x_ref), channel_id=1, source_target_pairs={{0,24},{8,0},{16,8},{24,16},{1,25},{9,1},{17,9},{25,17},{2,26},{10... | collective-permute-start | bytes 3145736 | tf_op jit(solution)/shard_map/ppermute | solution.py:224
  693.1 74.0 %collective-permute-start.8 = (bf16[1024,512]{1,0:T(8,128)(2,1)S(1)}, bf16[1024,512]{1,0:T(8,128)(2,1)S(1)}, u32[]{:S(2)}, u32[]{:S(2)}) collective-permute-start(bf16[1024,512]{1,0:T(8,128)(2,1)S(1)} %shard_map.109.x_ref), channel_id=1, source_target_pairs={{0,8},{8,16},{16,24},{24,0},{1,9},{9,17},{17,25},{25,1},{2,10},{10... | collective-permute-start | bytes 3145736 | tf_op jit(solution)/shard_map/ppermute | solution.py:223
  694.6 78.3 %collective-permute-start.7 = (bf16[1024,512]{1,0:T(8,128)(2,1)S(1)}, bf16[1024,512]{1,0:T(8,128)(2,1)S(1)}, u32[]{:S(2)}, u32[]{:S(2)}) collective-permute-start(bf16[1024,512]{1,0:T(8,128)(2,1)S(1)} %collective-permute-done.6.x_ref), channel_id=1, source_target_pairs={{0,8},{8,16},{16,24},{24,0},{1,9},{9,17},{17,25},{25,1},{2,10},{10... | collective-permute-start | bytes 3145736 | tf_op jit(solution)/shard_map/ppermute | solution.py:228
  713.6 67.4 %collective-permute-start.5 = (bf16[1024,512]{1,0:T(8,128)(2,1)S(1)}, bf16[1024,512]{1,0:T(8,128)(2,1)S(1)}, u32[]{:S(2)}, u32[]{:S(2)}) collective-permute-start(bf16[1024,512]{1,0:T(8,128)(2,1)S(1)} %collective-permute-done.4.x_ref), channel_id=1, source_target_pairs={{0,8},{8,16},{16,24},{24,0},{1,9},{9,17},{17,25},{25,1},{2,10},{10... | collective-permute-start | bytes 3145736 | tf_op jit(solution)/shard_map/ppermute | solution.py:228
  713.6 70.2 %collective-permute-start.3 = (bf16[1024,512]{1,0:T(8,128)(2,1)S(1)}, bf16[1024,512]{1,0:T(8,128)(2,1)S(1)}, u32[]{:S(2)}, u32[]{:S(2)}) collective-permute-start(bf16[1024,512]{1,0:T(8,128)(2,1)S(1)} %collective-permute-done.2.x_ref), channel_id=1, source_target_pairs={{0,24},{8,0},{16,8},{24,16},{1,25},{9,1},{17,9},{25,17},{2,26},{10... | collective-permute-start | bytes 3145736 | tf_op jit(solution)/shard_map/ppermute | solution.py:228
  735.1 51.7 %collective-permute-start.1 = (bf16[1024,512]{1,0:T(8,128)(2,1)S(1)}, bf16[1024,512]{1,0:T(8,128)(2,1)S(1)}, u32[]{:S(2)}, u32[]{:S(2)}) collective-permute-start(bf16[1024,512]{1,0:T(8,128)(2,1)S(1)} %collective-permute-done.x_ref), channel_id=1, source_target_pairs={{0,24},{8,0},{16,8},{24,16},{1,25},{9,1},{17,9},{25,17},{2,26},{10... | collective-permute-start | bytes 3145736 | tf_op jit(solution)/shard_map/ppermute | solution.py:228
Sparse Core Ops, SparseCore 0:
  9.4 91.2 all-gather.8
  102.8 282.4 all-gather.12
  387.4 129.4 all-gather.14
  518.8 107.7 all-gather.10

commit v2 on v1

--- a/solution.py
+++ b/solution.py
@@ -4,6 +4,7 @@
 import jax.numpy as jnp
 from jax import lax
 from jax.experimental import pallas as pl
+from jax.experimental.layout import Layout, with_layout_constraint
 from jax.experimental.pallas import tpu as pltpu
 from jax.sharding import PartitionSpec as P
 
@@ -72,15 +73,28 @@
             in_specs=[spec(0), spec(1), spec(2)],
             out_specs=pl.BlockSpec((1, seq_len, block), lambda s, g, h, lens: (s, 0, g * per + h)),
         ),
-        compiler_params=pltpu.CompilerParams(vmem_limit_bytes=40 * 1024 * 1024),
+        compiler_params=pltpu.CompilerParams(vmem_limit_bytes=60 * 1024 * 1024),
         cost_estimate=pl.CostEstimate(flops=16 * seqs * seq_len * seq_len * width, bytes_accessed=8 * seqs * seq_len * width, transcendentals=seqs * seq_len * seq_len * width // head_dim),
     )(lens, qkv, qkv, qkv)
 
 
-def mm_kernel(relu, steps, x_ref, w_ref, b_ref, *refs):
-    resid_ref = refs[0] if len(refs) == 3 else None
+def mm_kernel(relu, steps, has_resid, has_norm, x_ref, w_ref, b_ref, *refs):
+    resid_ref = refs[0] if has_resid else None
     o_ref, acc_ref = refs[-2:]
     k = pl.program_id(1)
+    if has_norm:
+        ln_ref, raw_ref, x_ref = refs[0], x_ref, acc_ref
+        chunk = 128
+
+        @pl.when(pl.program_id(0) == 0)
+        def _():
+            def normalise(i, carry):
+                r = pl.ds(pl.multiple_of(i * chunk, chunk), chunk)
+                x_ref[r, :] = layer_norm(raw_ref[r, :], ln_ref[0:1, :], ln_ref[1:2, :])
+                return carry
+
+            lax.fori_loop(0, raw_ref.shape[0] // chunk, normalise, 0)
+
     rows = x_ref.shape[0]
     w = w_ref[...].reshape(-1, w_ref.shape[2])
     half = min(512, rows)
@@ -107,7 +121,7 @@
             o_ref[r, :] = acc_ref[r, :].astype(o_ref.dtype)
 
 
-def matmul(x, w, bias, n, steps, w_block, w_index, resid=None, relu=False, first=0):
+def matmul(x, w, bias, n, steps, w_block, w_index, resid=None, relu=False, first=0, tiles=None, norm=None, vmem=60):
     rows, depth = x.shape
     tile = w_block[2]
     in_specs = [
@@ -119,42 +133,241 @@
     if resid is not None:
         in_specs.append(pl.BlockSpec((rows, tile), lambda j, k: (0, first + j)))
         args.append(resid)
+    scratch = pltpu.VMEM((rows, tile) if steps > 1 else (8, 128), jnp.float32)
+    if norm is not None:
+        in_specs.append(pl.BlockSpec((2, depth), lambda j, k: (0, 0)))
+        args.append(norm)
+        scratch = pltpu.VMEM((rows, depth), jnp.bfloat16)
+    tiles = tiles or n // tile
     return pl.pallas_call(
-        functools.partial(mm_kernel, relu, steps),
+        functools.partial(mm_kernel, relu, steps, resid is not None, norm is not None),
         out_shape=jax.ShapeDtypeStruct((rows, n), jnp.bfloat16),
-        grid=(n // tile, steps),
+        grid=(tiles, steps),
         in_specs=in_specs,
         out_specs=pl.BlockSpec((rows, tile), lambda j, k: (0, j)),
-        scratch_shapes=[pltpu.VMEM((rows, tile) if steps > 1 else (8, 128), jnp.float32)],
-        compiler_params=pltpu.CompilerParams(vmem_limit_bytes=48 * 1024 * 1024),
-        cost_estimate=pl.CostEstimate(flops=2 * rows * depth * n, bytes_accessed=2 * (depth * n + rows * (depth + n)), transcendentals=0),
+        scratch_shapes=[scratch],
+        compiler_params=pltpu.CompilerParams(vmem_limit_bytes=vmem * 1024 * 1024),
+        cost_estimate=pl.CostEstimate(flops=2 * rows * depth * tiles * tile, bytes_accessed=2 * (depth * tiles * tile + rows * (depth + tiles * tile)), transcendentals=0),
     )(*args)
 
 
-def place(out, x, step, column, size, total, width):
-    rows, tile = x.shape
-    piece = rows // 4
-
-    def kernel(x_ref, *refs):
-        o_ref, sem = refs[-2:]
-        owner = lax.rem(lax.axis_index('tp') + step + size, size)
-        row = pl.multiple_of(owner * rows + pl.program_id(0) * piece, piece)
-        copy = pltpu.make_async_copy(x_ref, o_ref.at[pl.ds(row, piece), pl.ds(column * tile, tile)], sem)
-        copy.start()
-        copy.wait()
+def place(out, blocks, size, total, width):
+    n = len(blocks)
+    rows, tile = blocks[0][2].shape
+
+    def kernel(*refs):
+        o_ref, sems = refs[-2:]
+        copies = []
+        for i, (step, column, _) in enumerate(blocks):
+            owner = lax.rem(lax.axis_index('tp') + step + size, size)
+            row = pl.multiple_of(owner * rows, rows)
+            copy = pltpu.make_async_copy(refs[i], o_ref.at[pl.ds(row, rows), pl.ds(column * tile, tile)], sems.at[i])
+            copy.start()
+            copies.append(copy)
+        for copy in copies:
+            copy.wait()
 
     whole = pl.BlockSpec(memory_space=pltpu.HBM)
+    args = [x for _, _, x in blocks] + ([] if out is None else [out])
     return pl.pallas_call(
         kernel,
-        out_shape=jax.ShapeDtypeStruct((total, width), x.dtype),
-        grid=(rows // piece,),
-        in_specs=[pl.BlockSpec((piece, tile), lambda i: (i, 0))] + ([] if out is None else [whole]),
+        out_shape=jax.ShapeDtypeStruct((total, width), args[0].dtype),
+        in_specs=[pl.BlockSpec(memory_space=pltpu.VMEM)] * n + ([] if out is None else [whole]),
         out_specs=whole,
-        scratch_shapes=[pltpu.SemaphoreType.DMA],
-        input_output_aliases={} if out is None else {1: 0},
-        compiler_params=pltpu.CompilerParams(vmem_limit_bytes=8 * 1024 * 1024),
-        cost_estimate=pl.CostEstimate(flops=x.size, bytes_accessed=4 * x.size, transcendentals=0),
-    )(*([x] if out is None else [x, out]))
+        scratch_shapes=[pltpu.SemaphoreType.DMA((n,))],
+        input_output_aliases={} if out is None else {n: 0},
+        compiler_params=pltpu.CompilerParams(vmem_limit_bytes=24 * 1024 * 1024),
+        cost_estimate=pl.CostEstimate(flops=n * rows * tile, bytes_accessed=4 * n * rows * tile, transcendentals=0),
+    )(*args)
+
+
+def gather_kernel(ny, nx, loads, n_in, *refs):
+    ins = refs[:n_in]
+    small_ref = refs[n_in]
+    out, small_out, *packed = refs[n_in + 1:n_in + 1 + 2 + len(loads) - 1]
+    rest = refs[n_in + 1 + 2 + len(loads) - 1:]
+    bufs, (load_sem, store_sem, send_sem, recv_sem, small_send, small_recv) = rest[:len(loads)], rest[len(loads):]
+    shard = bufs[0]
+    rows = shard.shape[0]
+    y = lax.axis_index('tp')
+    f = lax.axis_index('fsdp')
+    x = lax.div(f, 2)
+    core = lax.rem(f, 2)
+    at_y = lambda d: lax.rem(y + d + ny, ny)
+    at_x = lambda d: lax.rem(x + d + nx, nx)
+    slot = lambda dy, dx: (at_y(dy) * nx + at_x(dx)) * 2 + core
+    near = lambda dim, d: {'tp': at_y(d), 'fsdp': f} if dim == 'y' else {'tp': y, 'fsdp': at_x(d) * 2 + core}
+    partner = {'tp': y, 'fsdp': x * 2 + 1 - core}
+
+    barrier = pltpu.get_barrier_semaphore()
+    for dev in (near('x', 1), near('x', -1), near('y', 1), near('y', -1), partner):
+        pl.semaphore_signal(barrier, inc=1, device_id=dev, device_id_type=pl.DeviceIdType.MESH)
+
+    fills = []
+    for b, pieces in enumerate(loads):
+        for which, layer, c0, width, d0 in pieces:
+            src = ins[which] if layer is None else ins[which].at[layer]
+            fills.append((b, pltpu.make_async_copy(src.at[:, pl.ds(c0, width)], bufs[b].at[:, pl.ds(d0, width)], load_sem.at[len(fills)])))
+    for _, fill in fills:
+        fill.start()
+    for b, fill in fills:
+        if b == 0:
+            fill.wait()
+    stores = [pltpu.make_async_copy(shard, out.at[slot(0, 0)], store_sem.at[0]),
+              pltpu.make_async_copy(small_ref, small_out.at[core, y, x], store_sem.at[1])]
+    for store in stores:
+        store.start()
+    pl.semaphore_wait(barrier, 5)
+
+    sends = {}
+    order = []
+
+    def send(key, dev, dp, dq, r0, n):
+        colour = key[0]
+        where = slot(dq, dp) if colour == 0 else slot(dp, dq)
+        r = pl.ds(colour * (rows // 2) + r0, n)
+        src = shard.at[r] if (dp, dq) == (0, 0) else out.at[where, r]
+        i = len(order)
+        copy = pltpu.make_async_remote_copy(src, out.at[where, r], send_sem.at[i], recv_sem.at[i], device_id=dev, device_id_type=pl.DeviceIdType.MESH)
+        copy.start()
+        sends[key] = copy
+        order.append(key)
+
+    half, quarter = rows // 2, rows // 4
+    dims = ('xy', 'yx')
+    got = lambda *key: sends[key].wait_recv()
+
+    def full(c, phase, dp):
+        for d in (1, -1):
+            send((c, phase, dp, d, 'full'), near(dims[c][phase], d), dp, 0, 0, half)
+
+    def onward(c, phase, dp):
+        for d, r0 in ((1, 0), (-1, quarter)):
+            pos = (-d, 0) if phase == 0 else (dp, -d)
+            send((c, phase, dp, d, 'part'), near(dims[c][phase], d), *pos, r0, quarter)
+
+    def wait_full(c, phase, dp):
+        got(c, phase, dp, 1, 'full')
+        got(c, phase, dp, -1, 'full')
+
+    def wait_part(c, phase, dp):
+        got(c, phase, dp, 1, 'part')
+        got(c, phase, dp, -1, 'part')
+
+    def across(c, dp, dq):
+        send((c, 'core', dp, dq), partner, dp, dq, 0, half)
+
+    both = (0, 1)
+    smalls = []
+
+    def small(src, dst, dev):
+        i = len(smalls)
+        copy = pltpu.make_async_remote_copy(src, dst, small_send.at[i], small_recv.at[i], device_id=dev, device_id_type=pl.DeviceIdType.MESH)
+        copy.start()
+        smalls.append(copy)
+
+    mine = small_out.at[core, y, x]
+    for d in (1, -1):
+        small(small_ref, mine, near('x', d))
+    for c in both:
+        full(c, 0, 0)
+    for c in both:
+        full(c, 1, 0)
+    for c in both:
+        across(c, 0, 0)
+    for c in both:
+        wait_full(c, 0, 0)
+        onward(c, 0, 0)
+    for dp in (-1, 1):
+        for c in both:
+            full(c, 1, dp)
+            across(c, dp, 0)
+    smalls[0].wait_recv()
+    smalls[1].wait_recv()
+    left = small_out.at[core, y, at_x(-1)]
+    small(left, left, near('x', 1))
+    for b, fill in fills:
+        if b > 0:
+            fill.wait()
+    for b in range(1, len(loads)):
+        stores.append(pltpu.make_async_copy(bufs[b], packed[b - 1], store_sem.at[1 + b]))
+        stores[-1].start()
+    for c in both:
+        wait_full(c, 1, 0)
+        onward(c, 1, 0)
+        across(c, 0, -1)
+        across(c, 0, 1)
+    for c in both:
+        wait_part(c, 0, 0)
+        full(c, 1, 2)
+        across(c, 2, 0)
+    for dp in (-1, 1):
+        for c in both:
+            wait_full(c, 1, dp)
+            onward(c, 1, dp)
+            across(c, dp, -1)
+            across(c, dp, 1)
+        if dp == -1:
+            smalls[2].wait_recv()
+            stores[1].wait()
+            row = small_out.at[core, y]
+            for d in (1, -1):
+                small(row, row, near('y', d))
+        else:
+            smalls[3].wait_recv()
+            smalls[4].wait_recv()
+            below = small_out.at[core, at_y(-1)]
+            small(below, below, near('y', 1))
+    for c in both:
+        wait_part(c, 1, 0)
+        across(c, 0, 2)
+    for c in both:
+        wait_full(c, 1, 2)
+        onward(c, 1, 2)
+        across(c, 2, -1)
+        across(c, 2, 1)
+    smalls[5].wait_recv()
+    small(small_out.at[core], small_out.at[core], partner)
+    for dp in (-1, 1, 2):
+        for c in both:
+            wait_part(c, 1, dp)
+            across(c, dp, 2)
+    for key in order:
+        if key[1] == 'core':
+            sends[key].wait_recv()
+    smalls[6].wait_recv()
+    for key in order:
+        sends[key].wait_send()
+    for copy in smalls:
+        copy.wait_send()
+    for i, store in enumerate(stores):
+        if i != 1:
+            store.wait()
+
+
+def gather_first(ny, nx, arrays, small, loads):
+    rows = arrays[0].shape[-2]
+    widths = [sum(p[3] for p in pieces) for pieces in loads]
+    hbm = pl.BlockSpec(memory_space=pltpu.HBM)
+    shapes = [jax.ShapeDtypeStruct((ny * nx * 2, rows, widths[0]), jnp.bfloat16), jax.ShapeDtypeStruct((2, ny, nx) + small.shape, small.dtype)]
+    shapes += [jax.ShapeDtypeStruct((rows, w), jnp.bfloat16) for w in widths[1:]]
+    copies = 2 * (4 + 16 + 16)
+    return pl.pallas_call(
+        functools.partial(gather_kernel, ny, nx, loads, len(arrays)),
+        out_shape=shapes,
+        in_specs=[hbm] * len(arrays) + [pl.BlockSpec(memory_space=pltpu.VMEM)],
+        out_specs=[hbm] * len(shapes),
+        scratch_shapes=[pltpu.VMEM((rows, w), jnp.bfloat16) for w in widths] + [
+            pltpu.SemaphoreType.DMA((sum(len(p) for p in loads),)),
+            pltpu.SemaphoreType.DMA((1 + len(loads),)),
+            pltpu.SemaphoreType.DMA((copies,)),
+            pltpu.SemaphoreType.DMA((copies,)),
+            pltpu.SemaphoreType.DMA((7,)),
+            pltpu.SemaphoreType.DMA((7,)),
+        ],
+        compiler_params=pltpu.CompilerParams(collective_id=0, has_side_effects=True, vmem_limit_bytes=32 * 1024 * 1024),
+        cost_estimate=pl.CostEstimate(flops=2 * 10 ** 11, bytes_accessed=2 * ny * nx * 2 * rows * widths[0] * 2, transcendentals=0),
+    )(*arrays, small)
 
 
 def solution(mesh):
@@ -173,46 +386,55 @@
         me = lax.axis_index('tp')
 
         def gather(x):
-            return lax.all_gather(x, BOTH, axis=0, tiled=False)
+            return lax.all_gather(with_layout_constraint(x, Layout(major_to_minor=tuple(range(x.ndim)))), BOTH, axis=0, tiled=False)
 
         qkv_loc = [w_qkv[l].reshape(rows, 3 * share) for l in range(n_layers)]
         groups = rows // proj_rows
         proj_loc = [w_proj[l].reshape(proj_rows, groups, -1).transpose(1, 0, 2).reshape(rows, -1) for l in range(n_layers)]
         assert proj_loc[0].shape[1] == TILE and n_layers == 2
-        g1 = gather(qkv_loc[0])
-        g2 = gather(jnp.concatenate([w_up[0], w_down[0], qkv_loc[1], proj_loc[0]], axis=1))
-        g3 = gather(jnp.concatenate([w_up[1], proj_loc[1]], axis=1))
-        g4 = gather(w_down[1])
         wide_tiles = d_model // TILE
         ff_tiles = ff // TILE
-        qkv_at = [(g1, 0), (g2, ff_tiles + wide_tiles)]
-        proj_at = [(g2, ff_tiles + wide_tiles + 3 * share // TILE), (g3, ff_tiles)]
-        up_at = [(g2, 0), (g3, 0)]
-        down_at = [(g2, ff_tiles), (g4, 0)]
-
-        small = gather(jnp.concatenate([b_qkv.reshape(n_layers, -1), b_up], axis=1)).astype(jnp.float32)
-        small = small.reshape(tp, fs, n_layers, -1)
+        qkv_tiles = 3 * share // TILE
+        f32 = jnp.float32
+        small = jnp.concatenate([v.astype(f32).reshape(-1) for v in (ln_params, b_resid, b_qkv, b_up)])
+        used = small.size
+        small = jnp.pad(small, (0, -used % 1024)).reshape(-1, 128)
+        loads = (
+            ((0, 0, 0, ff, 0), (1, 0, 0, d_model, ff), (2, None, 0, 3 * share, ff + d_model), (4, None, 0, TILE, ff + d_model + 3 * share)),
+            ((0, 1, 0, ff, 0), (3, None, 0, 3 * share, ff), (5, None, 0, TILE, ff + 3 * share)),
+        )
+        g1, small, local2 = gather_first(tp, fs // 2, (w_up, w_down, qkv_loc[0], qkv_loc[1], proj_loc[0], proj_loc[1]), small, loads)
+        g2 = gather(local2)
+        g3 = gather(lax.optimization_barrier((w_down[1], local2))[0])
+        qkv_at = [(g1, ff_tiles + wide_tiles), (g2, ff_tiles)]
+        proj_at = [(g1, ff_tiles + wide_tiles + qkv_tiles), (g2, ff_tiles + qkv_tiles)]
+        down_at = [(g1, ff_tiles), (g3, 0)]
+
+        small = small.reshape(2, tp, fs // 2, -1).transpose(1, 2, 0, 3).reshape(tp, fs, -1)
         piece = share // fs
-        qkv_bias = small[..., :3 * piece].reshape(tp, fs, n_layers, 3, piece).transpose(2, 0, 3, 1, 4).reshape(n_layers, -1)
-        up_bias = small[..., 3 * piece:].transpose(2, 0, 1, 3).reshape(n_layers, -1)
-        wide = lax.all_gather(jnp.concatenate([ln_params, b_resid.astype(jnp.float32)], axis=1), 'fsdp', axis=2, tiled=True)
+        cuts = [0]
+        for v in (ln_params, b_resid, b_qkv, b_up):
+            cuts.append(cuts[-1] + v.size)
+        ln_full = small[0, :, :cuts[1]].reshape((fs,) + ln_params.shape).transpose(1, 2, 0, 3).reshape(n_layers, ln_params.shape[1], -1)
+        resid = small[0, :, cuts[1]:cuts[2]].reshape((fs,) + b_resid.shape).transpose(1, 2, 0, 3).reshape(n_layers, b_resid.shape[1], -1)
+        wide = jnp.concatenate([ln_full, resid], axis=1)
+        qkv_bias = small[..., cuts[2]:cuts[3]].reshape(tp, fs, n_layers, 3, piece).transpose(2, 0, 3, 1, 4).reshape(n_layers, -1)
+        up_bias = small[..., cuts[3]:cuts[4]].reshape(tp, fs, n_layers, -1).transpose(2, 0, 1, 3).reshape(n_layers, -1)
 
         current = lax.dynamic_slice_in_dim(hidden, me * my_seqs, my_seqs, 0).reshape(my_seqs * seq_len, d_model)
         lens = lax.dynamic_slice_in_dim(seq_lens, me * my_seqs, my_seqs, 0)
 
-        per = 3 * share // TILE
         for l in range(n_layers):
-            normed = layer_norm(current, wide[l, 0], wide[l, 1])
             w, c0 = qkv_at[l]
-            qkv = matmul(normed, w, qkv_bias[l], tp * 3 * share, 1, (fs, rows, TILE), lambda j, k, c0=c0: (j // per, 0, c0 + j % per))
+            qkv = matmul(current, w, qkv_bias[l], tp * 3 * share, 1, (fs, rows, TILE), lambda j, k, c0=c0: (j // qkv_tiles, 0, c0 + j % qkv_tiles), norm=wide[l, :2])
             context = attend(qkv.reshape(my_seqs, seq_len, -1), lens, share, head_dim)
             w, c0 = proj_at[l]
             mid = matmul(context.reshape(my_seqs * seq_len, -1), w, wide[l, 4], d_model, 1, (tp * fs, proj_rows, TILE), lambda j, k, c0=c0: (0, j, c0), resid=current)
-            normed_mid = layer_norm(mid, wide[l, 2], wide[l, 3])
-            w, c0 = up_at[l]
-            u = matmul(normed_mid, w, up_bias[l], tp * ff, 1, (fs, rows, TILE), lambda j, k, c0=c0: (j // ff_tiles, 0, c0 + j % ff_tiles), relu=True)
+            u = matmul(mid, (g1, g2)[l], up_bias[l], tp * ff, 1, (fs, rows, TILE), lambda j, k: (j // ff_tiles, 0, j % ff_tiles), relu=True, norm=wide[l, 2:4])
             w, c0 = down_at[l]
-            down = lambda first, n: matmul(u, w, wide[l, 5], n, tp, (fs, rows, TILE), lambda j, k: (k, 0, c0 + first + j), resid=mid, first=first)
+            block = 2 * TILE if l == 0 else TILE
+            steps, vmem = (2 * tp, 60) if l == 0 else (tp, 48)
+            down = lambda first, n: matmul(u, w, wide[l, 5], n, steps, (tp * fs // steps, rows, block), lambda j, k: (k, 0, c0 * TILE // block + first + j), resid=mid, first=first, vmem=vmem)
             if l + 1 < n_layers:
                 current = down(0, d_model)
         plus = [(i, (i + 1) % tp) for i in range(tp)]
@@ -226,9 +448,12 @@
         for j in range(wide_tiles):
             here, perm = (blocks[3 * j + 1], plus) if j < wide_tiles // 2 else (blocks[3 * j + 2], minus)
             blocks.append((2, j, lax.ppermute(here[2], 'tp', perm)))
+        near = 3 * wide_tiles
         out = None
-        for step, j, x in blocks:
-            out = place(out, x, step, j, tp, tp * my_seqs * seq_len, d_model)
+        total = tp * my_seqs * seq_len
+        pick = lambda *which: [blocks[i] for i in which]
+        for group in (pick(*range(6)), pick(*range(6, near)), pick(near, near + 2), pick(near + 1, near + 3)):
+            out = place(out, group, tp, total, d_model)
         return out.reshape(hidden.shape)
 
     return jax.shard_map(per_device, mesh=mesh, in_specs=in_specs, out_specs=rows_spec, check_vma=False)

time: 802 us -> 771 us (0.961)
  Pallas kernels: 378 us -> 633 us
  waiting for transfers between devices: 284 us -> 88 us
  blocking collectives: 57.6 us -> 0 us
  other arithmetic: 27.8 us -> 1.37 us
    pallas_call x27 -> x16, Pallas kernels: 322 us -> 575 us  [the longest x11 294 us: matmul(): pl.pallas_call(functools.partial(mm_kernel, relu, steps, resid is not Non...]
    all_gather x4 -> x2, waiting for transfers between devices: 240 us -> 8.2 us  [gather(): lax.all_gather(with_layout_constraint(x, Layout(major_to_minor=tuple(rang...]
    all_gather x2 -> x0, blocking collectives: 57.6 us -> none  [the longest x1 32.5 us: gather(): return lax.all_gather(x, BOTH, axis=0, tiled=False)]
    ppermute x4, waiting for transfers between devices: 5.34 us -> 38 us  [per_device(): blocks.append((2, j, lax.ppermute(here[2], 'tp', perm)))]
    ppermute x4, waiting for transfers between devices: 18.8 us -> 41.5 us  [per_device(): left = lax.ppermute(own, 'tp', minus)]
    ppermute x4, waiting for transfers between devices: 19 us -> 0.23 us  [per_device(): right = lax.ppermute(own, 'tp', plus)]
    reduce_sum x8 -> x0, other arithmetic: 13.9 us -> none  [the longest x4 7.18 us: layer_norm(): row_var = jnp.mean(centered * centered, axis=-1, keepdims=True)]
    convert_element_type x5 -> x0, other arithmetic: 10.7 us -> none  [the longest x4 10.7 us: layer_norm(): (centered * lax.rsqrt(row_var + 1e-05) * ln_gain + ln_shift).astype(jnp.b...]
  transfers between devices with their start and end apart: 16 -> 14, of which waited for: 6 -> 8; matrix products, arithmetic and copies ran while one was open for 4% -> 2% of each run, Pallas kernels for 45% -> 45%
where the time goes in v2:
time: 771 us; the launch traced here: 769 us
  Pallas kernels  633 us (82%)
  waiting for transfers between devices  88 us (11%)
  local copies, waits for them, and re-layouts  23 us (3%)
  between operations  13.7 us (2%)
  starting transfers between devices  10.2 us (1%)
    pallas_call x11, Pallas kernels, matmul(): pl.pallas_call(functools.partial(mm_kernel, relu, steps, resid is not Non...  294 us
    pallas_call x1, Pallas kernels, gather_first(): pl.pallas_call(functools.partial(gather_kernel, ny, nx, loads, len(arrays...  273 us
    pallas_call x2, Pallas kernels, attend(): pl.pallas_call(functools.partial(attn_kernel, head_dim, block // head_dim...  57.8 us
    ppermute x4, waiting for transfers between devices, per_device(): left = lax.ppermute(own, 'tp', minus)  41.5 us
    ppermute x4, waiting for transfers between devices, per_device(): blocks.append((2, j, lax.ppermute(here[2], 'tp', perm)))  38 us
  transfers between devices with their start and end apart: 14, of which 8 were waited for; matrix products, arithmetic and copies ran while one was open for 2% of the time, Pallas kernels for 45%

profile of v2, /device:TPU:97, one launch (start us, length us, event | category | flops | bytes accessed | tf_op | source)
XLA Modules:
  0.0 769.0 jit_solution(8447578681109805872)
XLA Ops:
  6.6 1.5 fusion.1
  8.0 0.3 copy.32.refs_2_
  8.3 0.3 copy.33.refs_3_
  8.6 1.1 fusion.2
  9.7 0.2 reshape_squeeze.35
  9.9 0.2 reshape_squeeze.36
  10.1 0.7 copy.42
  10.8 0.7 convert_bitcast_fusion
  11.5 0.7 copy.31
  12.2 0.1 reshape.97
  12.3 0.7 convert_bitcast_fusion.1
  13.0 1.6 copy-done.1
  14.6 1.6 copy-done.2
  16.2 272.5 %shard_map.100 = (bf16[32,256,6144]{2,1,0:T(8,128)(2,1)}, f32[2,4,4,32,128]{4,3,2,1,0:T(8,128)S(1)}, bf16[256,4096]{1,0:T(8,128)(2,1)}) custom-call(bf16[2,256,2048]{2,1,0:T(8,128)(2,1)S(1)} %copy-done.2, bf16[2,256,2048]{2,1,0:T(8,128)(2,1)S(1)} %copy-done.1, bf16[256,1536]{1,0:T(8,128)(2,1)S(1)} %copy.32.refs_2_, bf16[256,1536]{1,0:T(8,128)(2,1)S(1)} %copy.33.refs_3_, ...), custom_call_target="tpu_custom_call" | custom-call | flops 199999995904 | bytes 201326592 | tf_op jit(solution)/shard_map/pallas_call | solution.py:355
  288.9 2.3 slice_bitcast_fusion
  291.2 0.2 reshape.83
  291.4 0.3 copy.34
  291.8 0.2 slice_reduce_fusion
  292.0 0.1 reshape.85
  292.2 0.7 slice.84.b_ref
  293.1 0.7 slice.95.b_ref
  293.8 0.7 dynamic_slice.6.lens_ref
  294.5 0.7 fusion.4
  295.1 5.3 constant_dynamic-slice_fusion
  300.4 0.6 slice_bitcast_fusion.5
  301.0 0.6 slice_bitcast_fusion.1
  301.7 35.8 %shard_map.101 = bf16[1024,6144]{1,0:T(8,128)(2,1)} custom-call(bf16[1024,2048]{1,0:T(8,128)(2,1)} %bitcast.77, bf16[32,256,6144]{2,1,0:T(8,128)(2,1)} %get-tuple-element.9.w_ref, f32[1,6144]{1,0:T(1,128)} %slice.84.b_ref, f32[2,2048]{1,0:T(2,128)} %get-tuple-element.22.refs_0_), custom_call_target="tpu_custom_call" | custom-call | flops 25769803776 | bytes 41943040 | tf_op jit(solution)/shard_map/pallas_call | solution.py:142
  337.4 28.8 %shard_map.102 = bf16[2,512,2048]{2,1,0:T(8,128)(2,1)} custom-call(s32[2]{0:T(128)} %dynamic_slice.6.lens_ref, bf16[2,512,6144]{2,1,0:T(8,128)(2,1)} %bitcast.79, bf16[2,512,6144]{2,1,0:T(8,128)(2,1)} %bitcast.80, bf16[2,512,6144]{2,1,0:T(8,128)(2,1)} %bitcast.81), custom_call_target="tpu_custom_call" | custom-call | flops 17179869184 | bytes 16777216 | tf_op jit(solution)/shard_map/pallas_call | solution.py:67
  366.2 13.9 %shard_map.103.x_ref.refs_0_ = bf16[1024,2048]{1,0:T(8,128)(2,1)} custom-call(bf16[1024,2048]{1,0:T(8,128)(2,1)} %bitcast.82, bf16[32,256,6144]{2,1,0:T(8,128)(2,1)} %get-tuple-element.9.w_ref, f32[1,2048]{1,0:T(1,128)} %get-tuple-element.28.b_ref, bf16[1024,2048]{1,0:T(8,128)(2,1)} %bitcast.78), custom_call_target="tpu_custom_call" | custom-call | flops 8589934592 | bytes 16777216 | tf_op jit(solution)/shard_map/pallas_call | solution.py:142
  380.1 45.3 %shard_map.104.x_ref = bf16[1024,8192]{1,0:T(8,128)(2,1)} custom-call(bf16[1024,2048]{1,0:T(8,128)(2,1)} %shard_map.103.x_ref.refs_0_, bf16[32,256,6144]{2,1,0:T(8,128)(2,1)} %get-tuple-element.9.w_ref, f32[1,8192]{1,0:T(1,128)} %bitcast.96, f32[2,2048]{1,0:T(2,128)} %get-tuple-element.21.refs_0_), custom_call_target="tpu_custom_call" | custom-call | flops 34359738368 | bytes 54525952 | tf_op jit(solution)/shard_map/pallas_call | solution.py:142
  425.4 48.4 %shard_map.105.x_ref.refs_0_ = bf16[1024,2048]{1,0:T(8,128)(2,1)} custom-call(bf16[1024,8192]{1,0:T(8,128)(2,1)} %shard_map.104.x_ref, bf16[32,256,6144]{2,1,0:T(8,128)(2,1)} %get-tuple-element.9.w_ref, f32[1,2048]{1,0:T(1,128)} %get-tuple-element.27.b_ref, bf16[1024,2048]{1,0:T(8,128)(2,1)} %shard_map.103.x_ref.refs_0_), custom_call_target="tpu_custom_call" | custom-call | flops 34359738368 | bytes 54525952 | tf_op jit(solution)/shard_map/pallas_call | solution.py:142
  473.8 8.2 %all-gather.5.cloned.1.call-done = bf16[8192,4096]{1,0:T(8,128)(2,1)} async-done(((bf16[256,4096]{1,0:T(8,128)(2,1)}), bf16[8192,4096]{1,0:T(8,128)(2,1)}) %all-gather.5.cloned.1.call-update) | async-done | bytes 67108880 | tf_op jit(solution)/shard_map/all_gather | solution.py:389
  482.0 35.6 %shard_map.106 = bf16[1024,6144]{1,0:T(8,128)(2,1)} custom-call(bf16[1024,2048]{1,0:T(8,128)(2,1)} %shard_map.105.x_ref.refs_0_, bf16[32,256,4096]{2,1,0:T(8,128)(2,1)} %bitcast.22.w_ref, f32[1,6144]{1,0:T(1,128)} %slice.95.b_ref, f32[2,2048]{1,0:T(2,128)} %get-tuple-element.20.refs_0_), custom_call_target="tpu_custom_call" | custom-call | flops 25769803776 | bytes 41943040 | tf_op jit(solution)/shard_map/pallas_call | solution.py:142
  517.6 29.0 %shard_map.107 = bf16[2,512,2048]{2,1,0:T(8,128)(2,1)} custom-call(s32[2]{0:T(128)} %dynamic_slice.6.lens_ref, bf16[2,512,6144]{2,1,0:T(8,128)(2,1)} %bitcast.100, bf16[2,512,6144]{2,1,0:T(8,128)(2,1)} %bitcast.101, bf16[2,512,6144]{2,1,0:T(8,128)(2,1)} %bitcast.102), custom_call_target="tpu_custom_call" | custom-call | flops 17179869184 | bytes 16777216 | tf_op jit(solution)/shard_map/pallas_call | solution.py:67
  546.6 13.9 %shard_map.108.x_ref.refs_0_ = bf16[1024,2048]{1,0:T(8,128)(2,1)} custom-call(bf16[1024,2048]{1,0:T(8,128)(2,1)} %bitcast.83, bf16[32,256,4096]{2,1,0:T(8,128)(2,1)} %bitcast.22.w_ref, f32[1,2048]{1,0:T(1,128)} %get-tuple-element.26.b_ref, bf16[1024,2048]{1,0:T(8,128)(2,1)} %shard_map.105.x_ref.refs_0_), custom_call_target="tpu_custom_call" | custom-call | flops 8589934592 | bytes 16777216 | tf_op jit(solution)/shard_map/pallas_call | solution.py:142
  560.6 45.6 %shard_map.109.x_ref = bf16[1024,8192]{1,0:T(8,128)(2,1)} custom-call(bf16[1024,2048]{1,0:T(8,128)(2,1)} %shard_map.108.x_ref.refs_0_, bf16[32,256,4096]{2,1,0:T(8,128)(2,1)} %bitcast.22.w_ref, f32[1,8192]{1,0:T(1,128)} %bitcast.95, f32[2,2048]{1,0:T(2,128)} %get-tuple-element.19.refs_0_), custom_call_target="tpu_custom_call" | custom-call | flops 34359738368 | bytes 54525952 | tf_op jit(solution)/shard_map/pallas_call | solution.py:142
  606.2 2.2 copy-done
  608.4 13.9 %shard_map.112.refs_0_ = bf16[1024,512]{1,0:T(8,128)(2,1)S(1)} custom-call(bf16[1024,8192]{1,0:T(8,128)(2,1)} %shard_map.109.x_ref, bf16[32,256,2048]{2,1,0:T(8,128)(2,1)} %bitcast.73, f32[1,2048]{1,0:T(1,128)S(1)} %get-tuple-element.25.b_ref, bf16[1024,2048]{1,0:T(8,128)(2,1)S(1)} %copy-done), custom_call_target="tpu_custom_call" | custom-call | flops 8589934592 | bytes 26214400 | tf_op jit(solution)/shard_map/pallas_call | solution.py:142
  622.3 0.5 collective-permute-start.10
  622.7 1.1 collective-permute-start.4
  623.8 13.9 %shard_map.110.refs_3_ = bf16[1024,512]{1,0:T(8,128)(2,1)S(1)} custom-call(bf16[1024,8192]{1,0:T(8,128)(2,1)} %shard_map.109.x_ref, bf16[32,256,2048]{2,1,0:T(8,128)(2,1)} %bitcast.74, f32[1,2048]{1,0:T(1,128)S(1)} %get-tuple-element.25.b_ref, bf16[1024,2048]{1,0:T(8,128)(2,1)S(1)} %copy-done), custom_call_target="tpu_custom_call" | custom-call | flops 8589934592 | bytes 26214400 | tf_op jit(solution)/shard_map/pallas_call | solution.py:142
  637.8 0.1 collective-permute-start
  637.9 2.6 collective-permute-start.11
  640.5 13.9 %shard_map.113.refs_0_ = bf16[1024,512]{1,0:T(8,128)(2,1)S(1)} custom-call(bf16[1024,8192]{1,0:T(8,128)(2,1)} %shard_map.109.x_ref, bf16[32,256,2048]{2,1,0:T(8,128)(2,1)} %bitcast.75, f32[1,2048]{1,0:T(1,128)S(1)} %get-tuple-element.25.b_ref, bf16[1024,2048]{1,0:T(8,128)(2,1)S(1)} %copy-done), custom_call_target="tpu_custom_call" | custom-call | flops 8589934592 | bytes 26214400 | tf_op jit(solution)/shard_map/pallas_call | solution.py:142
  654.5 0.5 collective-permute-start.6
  654.9 13.9 %shard_map.111.refs_3_ = bf16[1024,512]{1,0:T(8,128)(2,1)S(1)} custom-call(bf16[1024,8192]{1,0:T(8,128)(2,1)} %shard_map.109.x_ref, bf16[32,256,2048]{2,1,0:T(8,128)(2,1)} %bitcast.76, f32[1,2048]{1,0:T(1,128)S(1)} %get-tuple-element.25.b_ref, bf16[1024,2048]{1,0:T(8,128)(2,1)S(1)} %copy-done), custom_call_target="tpu_custom_call" | custom-call | flops 8589934592 | bytes 26214400 | tf_op jit(solution)/shard_map/pallas_call | solution.py:142
  668.9 0.1 collective-permute-start.2
  669.0 1.4 collective-permute-start.8
  670.4 0.2 collective-permute-done.refs_4_
  670.6 0.9 collective-permute-start.9
  671.5 20.5 %collective-permute-done.6.refs_2_ = bf16[1024,512]{1,0:T(8,128)(2,1)S(1)} collective-permute-done((bf16[1024,512]{1,0:T(8,128)(2,1)S(1)}, bf16[1024,512]{1,0:T(8,128)(2,1)S(1)}, u32[]{:S(2)}, u32[]{:S(2)}) %collective-permute-start.6) | collective-permute-done | bytes 1048608 | tf_op jit(solution)/shard_map/ppermute | solution.py:446
  692.1 1.3 collective-permute-start.7
  693.4 0.1 collective-permute-start.5
  693.5 21.0 %collective-permute-done.2.refs_5_ = bf16[1024,512]{1,0:T(8,128)(2,1)S(1)} collective-permute-done((bf16[1024,512]{1,0:T(8,128)(2,1)S(1)}, bf16[1024,512]{1,0:T(8,128)(2,1)S(1)}, u32[]{:S(2)}, u32[]{:S(2)}) %collective-permute-start.2) | collective-permute-done | bytes 1048608 | tf_op jit(solution)/shard_map/ppermute | solution.py:446
  714.5 1.3 collective-permute-start.3
  715.9 0.1 collective-permute-start.1
  716.0 2.7 shard_map.114.refs_6_
  718.7 2.7 shard_map.115.refs_2_
  721.5 15.5 %collective-permute-done.7.refs_1_ = bf16[1024,512]{1,0:T(8,128)(2,1)S(1)} collective-permute-done((bf16[1024,512]{1,0:T(8,128)(2,1)S(1)}, bf16[1024,512]{1,0:T(8,128)(2,1)S(1)}, u32[]{:S(2)}, u32[]{:S(2)}) %collective-permute-start.7) | collective-permute-done | bytes 1048608 | tf_op jit(solution)/shard_map/ppermute | solution.py:450
  737.0 1.3 collective-permute-done.5.refs_0_
  738.3 1.3 shard_map.116.refs_2_
  739.7 19.8 %collective-permute-done.3.refs_1_ = bf16[1024,512]{1,0:T(8,128)(2,1)S(1)} collective-permute-done((bf16[1024,512]{1,0:T(8,128)(2,1)S(1)}, bf16[1024,512]{1,0:T(8,128)(2,1)S(1)}, u32[]{:S(2)}, u32[]{:S(2)}) %collective-permute-start.3) | collective-permute-done | bytes 1048608 | tf_op jit(solution)/shard_map/ppermute | solution.py:450
  759.5 1.3 collective-permute-done.1.refs_0_
  760.8 1.3 shard_map.117
  (31 shorter events, 0.6 us)
Async XLA Ops:
  6.5 475.5 %all-gather.5.cloned.1.call-start = ((), (), s32[]{:S(2)}) async-start(), calls=%async_computation | async-start | bytes 69206016 | tf_op jit(solution)/shard_map/all_gather | solution.py:389
  13.0 1.6 copy-start.1
  14.6 1.6 copy-start.2
  16.2 277.6 %copy-start.3 = (s32[8]{0:T(128)S(1)}, s32[8]{0:T(128)}, u32[]{:S(2)}) copy-start(s32[8]{0:T(128)} %param.11) | copy-start | bytes 100
  288.8 317.4 %all-gather.7.cloned.1.call-start = ((), (), s32[]{:S(2)}) async-start(), calls=%async_computation.1 | async-start | bytes 34603008 | tf_op jit(solution)/shard_map/all_gather | solution.py:389
  606.2 2.2 copy-start
  622.3 46.6 %collective-permute-start.10 = (bf16[1024,512]{1,0:T(8,128)(2,1)S(1)}, bf16[1024,512]{1,0:T(8,128)(2,1)S(1)}, u32[]{:S(2)}, u32[]{:S(2)}) collective-permute-start(bf16[1024,512]{1,0:T(8,128)(2,1)S(1)} %shard_map.112.refs_0_), channel_id=1, source_target_pairs={{0,24},{8,0},{16,8},{24,16},{1,25},{9,1},{17,9},{25,17},{2,26},{10... | collective-permute-start | bytes 3145736 | tf_op jit(solution)/shard_map/ppermute | solution.py:446
  622.7 46.3 %collective-permute-start.4 = (bf16[1024,512]{1,0:T(8,128)(2,1)S(1)}, bf16[1024,512]{1,0:T(8,128)(2,1)S(1)}, u32[]{:S(2)}, u32[]{:S(2)}) collective-permute-start(bf16[1024,512]{1,0:T(8,128)(2,1)S(1)} %shard_map.112.refs_0_), channel_id=1, source_target_pairs={{0,8},{8,16},{16,24},{24,0},{1,9},{9,17},{17,25},{25,1},{2,10},{10... | collective-permute-start | bytes 3145736 | tf_op jit(solution)/shard_map/ppermute | solution.py:445
  637.8 32.9 %collective-permute-start = (bf16[1024,512]{1,0:T(8,128)(2,1)S(1)}, bf16[1024,512]{1,0:T(8,128)(2,1)S(1)}, u32[]{:S(2)}, u32[]{:S(2)}) collective-permute-start(bf16[1024,512]{1,0:T(8,128)(2,1)S(1)} %shard_map.110.refs_3_), channel_id=1, source_target_pairs={{0,8},{8,16},{16,24},{24,0},{1,9},{9,17},{17,25},{25,1},{2,10},{10... | collective-permute-start | bytes 3145736 | tf_op jit(solution)/shard_map/ppermute | solution.py:445
  637.9 55.5 %collective-permute-start.11 = (bf16[1024,512]{1,0:T(8,128)(2,1)S(1)}, bf16[1024,512]{1,0:T(8,128)(2,1)S(1)}, u32[]{:S(2)}, u32[]{:S(2)}) collective-permute-start(bf16[1024,512]{1,0:T(8,128)(2,1)S(1)} %shard_map.110.refs_3_), channel_id=1, source_target_pairs={{0,24},{8,0},{16,8},{24,16},{1,25},{9,1},{17,9},{25,17},{2,26},{10... | collective-permute-start | bytes 3145736 | tf_op jit(solution)/shard_map/ppermute | solution.py:446
  654.5 37.6 %collective-permute-start.6 = (bf16[1024,512]{1,0:T(8,128)(2,1)S(1)}, bf16[1024,512]{1,0:T(8,128)(2,1)S(1)}, u32[]{:S(2)}, u32[]{:S(2)}) collective-permute-start(bf16[1024,512]{1,0:T(8,128)(2,1)S(1)} %shard_map.113.refs_0_), channel_id=1, source_target_pairs={{0,24},{8,0},{16,8},{24,16},{1,25},{9,1},{17,9},{25,17},{2,26},{10... | collective-permute-start | bytes 3145736 | tf_op jit(solution)/shard_map/ppermute | solution.py:446
  668.9 45.7 %collective-permute-start.2 = (bf16[1024,512]{1,0:T(8,128)(2,1)S(1)}, bf16[1024,512]{1,0:T(8,128)(2,1)S(1)}, u32[]{:S(2)}, u32[]{:S(2)}) collective-permute-start(bf16[1024,512]{1,0:T(8,128)(2,1)S(1)} %shard_map.111.refs_3_), channel_id=1, source_target_pairs={{0,24},{8,0},{16,8},{24,16},{1,25},{9,1},{17,9},{25,17},{2,26},{10... | collective-permute-start | bytes 3145736 | tf_op jit(solution)/shard_map/ppermute | solution.py:446
  669.0 46.9 %collective-permute-start.8 = (bf16[1024,512]{1,0:T(8,128)(2,1)S(1)}, bf16[1024,512]{1,0:T(8,128)(2,1)S(1)}, u32[]{:S(2)}, u32[]{:S(2)}) collective-permute-start(bf16[1024,512]{1,0:T(8,128)(2,1)S(1)} %shard_map.113.refs_0_), channel_id=1, source_target_pairs={{0,8},{8,16},{16,24},{24,0},{1,9},{9,17},{17,25},{25,1},{2,10},{10... | collective-permute-start | bytes 3145736 | tf_op jit(solution)/shard_map/ppermute | solution.py:445
  670.6 48.1 %collective-permute-start.9 = (bf16[1024,512]{1,0:T(8,128)(2,1)S(1)}, bf16[1024,512]{1,0:T(8,128)(2,1)S(1)}, u32[]{:S(2)}, u32[]{:S(2)}) collective-permute-start(bf16[1024,512]{1,0:T(8,128)(2,1)S(1)} %shard_map.111.refs_3_), channel_id=1, source_target_pairs={{0,8},{8,16},{16,24},{24,0},{1,9},{9,17},{17,25},{25,1},{2,10},{10... | collective-permute-start | bytes 3145736 | tf_op jit(solution)/shard_map/ppermute | solution.py:445
  692.1 44.9 %collective-permute-start.7 = (bf16[1024,512]{1,0:T(8,128)(2,1)S(1)}, bf16[1024,512]{1,0:T(8,128)(2,1)S(1)}, u32[]{:S(2)}, u32[]{:S(2)}) collective-permute-start(bf16[1024,512]{1,0:T(8,128)(2,1)S(1)} %collective-permute-done.6.refs_2_), channel_id=1, source_target_pairs={{0,24},{8,0},{16,8},{24,16},{1,25},{9,1},{17,9},{25,17},{2,26},{10... | collective-permute-start | bytes 3145736 | tf_op jit(solution)/shard_map/ppermute | solution.py:450
  693.4 44.9 %collective-permute-start.5 = (bf16[1024,512]{1,0:T(8,128)(2,1)S(1)}, bf16[1024,512]{1,0:T(8,128)(2,1)S(1)}, u32[]{:S(2)}, u32[]{:S(2)}) collective-permute-start(bf16[1024,512]{1,0:T(8,128)(2,1)S(1)} %collective-permute-done.4.refs_1_), channel_id=1, source_target_pairs={{0,8},{8,16},{16,24},{24,0},{1,9},{9,17},{17,25},{25,1},{2,10},{10... | collective-permute-start | bytes 3145736 | tf_op jit(solution)/shard_map/ppermute | solution.py:450
  714.5 44.9 %collective-permute-start.3 = (bf16[1024,512]{1,0:T(8,128)(2,1)S(1)}, bf16[1024,512]{1,0:T(8,128)(2,1)S(1)}, u32[]{:S(2)}, u32[]{:S(2)}) collective-permute-start(bf16[1024,512]{1,0:T(8,128)(2,1)S(1)} %collective-permute-done.2.refs_5_), channel_id=1, source_target_pairs={{0,24},{8,0},{16,8},{24,16},{1,25},{9,1},{17,9},{25,17},{2,26},{10... | collective-permute-start | bytes 3145736 | tf_op jit(solution)/shard_map/ppermute | solution.py:450
  715.9 44.9 %collective-permute-start.1 = (bf16[1024,512]{1,0:T(8,128)(2,1)S(1)}, bf16[1024,512]{1,0:T(8,128)(2,1)S(1)}, u32[]{:S(2)}, u32[]{:S(2)}) collective-permute-start(bf16[1024,512]{1,0:T(8,128)(2,1)S(1)} %collective-permute-done.refs_4_), channel_id=1, source_target_pairs={{0,8},{8,16},{16,24},{24,0},{1,9},{9,17},{17,25},{25,1},{2,10},{10... | collective-permute-start | bytes 3145736 | tf_op jit(solution)/shard_map/ppermute | solution.py:450
Sparse Core Ops, SparseCore 0:
  288.9 193.0 all-gather.4
  484.1 107.5 all-gather.6

commit v3 on v2

--- a/solution.py
+++ b/solution.py
@@ -181,12 +181,13 @@
     )(*args)
 
 
-def gather_kernel(ny, nx, loads, n_in, *refs):
+def gather_kernel(ny, nx, loads, n_in, own, *refs):
+    n_buf = len(loads) + own
     ins = refs[:n_in]
     small_ref = refs[n_in]
-    out, small_out, *packed = refs[n_in + 1:n_in + 1 + 2 + len(loads) - 1]
-    rest = refs[n_in + 1 + 2 + len(loads) - 1:]
-    bufs, (load_sem, store_sem, send_sem, recv_sem, small_send, small_recv) = rest[:len(loads)], rest[len(loads):]
+    out, small_out, *packed = refs[n_in + 1:n_in + 2 + n_buf]
+    rest = refs[n_in + 2 + n_buf:]
+    bufs, (load_sem, store_sem, send_sem, recv_sem, small_send, small_recv) = rest[:n_buf], rest[n_buf:]
     shard = bufs[0]
     rows = shard.shape[0]
     y = lax.axis_index('tp')
@@ -208,6 +209,9 @@
         for which, layer, c0, width, d0 in pieces:
             src = ins[which] if layer is None else ins[which].at[layer]
             fills.append((b, pltpu.make_async_copy(src.at[:, pl.ds(c0, width)], bufs[b].at[:, pl.ds(d0, width)], load_sem.at[len(fills)])))
+    if own:
+        mine = bufs[-1].shape[0]
+        fills.append((n_buf - 1, pltpu.make_async_copy(ins[-1].at[pl.ds(pl.multiple_of(y * mine, mine), mine)], bufs[-1], load_sem.at[len(fills)])))
     for _, fill in fills:
         fill.start()
     for b, fill in fills:
@@ -289,7 +293,7 @@
     for b, fill in fills:
         if b > 0:
             fill.wait()
-    for b in range(1, len(loads)):
+    for b in range(1, n_buf):
         stores.append(pltpu.make_async_copy(bufs[b], packed[b - 1], store_sem.at[1 + b]))
         stores[-1].start()
     for c in both:
@@ -345,28 +349,25 @@
             store.wait()
 
 
-def gather_first(ny, nx, arrays, small, loads):
+def gather_first(ny, nx, arrays, small, loads, own, collective_id):
     rows = arrays[0].shape[-2]
     widths = [sum(p[3] for p in pieces) for pieces in loads]
     hbm = pl.BlockSpec(memory_space=pltpu.HBM)
+    local = [(rows, w) for w in widths]
+    if own:
+        local.append((arrays[-1].shape[0] // ny, arrays[-1].shape[1]))
     shapes = [jax.ShapeDtypeStruct((ny * nx * 2, rows, widths[0]), jnp.bfloat16), jax.ShapeDtypeStruct((2, ny, nx) + small.shape, small.dtype)]
-    shapes += [jax.ShapeDtypeStruct((rows, w), jnp.bfloat16) for w in widths[1:]]
+    shapes += [jax.ShapeDtypeStruct(shape, jnp.bfloat16) for shape in local[1:]]
     copies = 2 * (4 + 16 + 16)
+    sizes = (sum(len(p) for p in loads) + own, 1 + len(local), copies, copies, 7, 7)
     return pl.pallas_call(
-        functools.partial(gather_kernel, ny, nx, loads, len(arrays)),
+        functools.partial(gather_kernel, ny, nx, loads, len(arrays), own),
         out_shape=shapes,
         in_specs=[hbm] * len(arrays) + [pl.BlockSpec(memory_space=pltpu.VMEM)],
         out_specs=[hbm] * len(shapes),
-        scratch_shapes=[pltpu.VMEM((rows, w), jnp.bfloat16) for w in widths] + [
-            pltpu.SemaphoreType.DMA((sum(len(p) for p in loads),)),
-            pltpu.SemaphoreType.DMA((1 + len(loads),)),
-            pltpu.SemaphoreType.DMA((copies,)),
-            pltpu.SemaphoreType.DMA((copies,)),
-            pltpu.SemaphoreType.DMA((7,)),
-            pltpu.SemaphoreType.DMA((7,)),
-        ],
-        compiler_params=pltpu.CompilerParams(collective_id=0, has_side_effects=True, vmem_limit_bytes=32 * 1024 * 1024),
-        cost_estimate=pl.CostEstimate(flops=2 * 10 ** 11, bytes_accessed=2 * ny * nx * 2 * rows * widths[0] * 2, transcendentals=0),
+        scratch_shapes=[pltpu.VMEM(shape, jnp.bfloat16) for shape in local] + [pltpu.SemaphoreType.DMA((n,)) for n in sizes],
+        compiler_params=pltpu.CompilerParams(collective_id=collective_id, has_side_effects=True, vmem_limit_bytes=60 * 1024 * 1024),
+        cost_estimate=pl.CostEstimate(flops=32 * rows * widths[0] * ny * nx, bytes_accessed=8 * ny * nx * rows * widths[0], transcendentals=0),
     )(*arrays, small)
 
 
@@ -400,14 +401,18 @@
         used = small.size
         small = jnp.pad(small, (0, -used % 1024)).reshape(-1, 128)
         loads = (
-            ((0, 0, 0, ff, 0), (1, 0, 0, d_model, ff), (2, None, 0, 3 * share, ff + d_model), (4, None, 0, TILE, ff + d_model + 3 * share)),
-            ((0, 1, 0, ff, 0), (3, None, 0, 3 * share, ff), (5, None, 0, TILE, ff + 3 * share)),
+            ((0, 0, 0, ff, 0), (1, 0, 0, d_model, ff), (2, None, 0, 3 * share, ff + d_model)),
+            ((0, 1, 0, ff, 0), (3, None, 0, 3 * share, ff), (4, None, 0, TILE, ff + 3 * share)),
+            ((1, 1, 0, d_model, 0),),
         )
-        g1, small, local2 = gather_first(tp, fs // 2, (w_up, w_down, qkv_loc[0], qkv_loc[1], proj_loc[0], proj_loc[1]), small, loads)
+        rows_all = hidden.reshape(-1, d_model)
+        g1, token, local2, local3, current = gather_first(tp, fs // 2, (w_up, w_down, qkv_loc[0], qkv_loc[1], proj_loc[1], rows_all), jnp.zeros((8, 128), f32), loads, 1, 0)
+        proj0, small, token, g1, local2, local3 = lax.optimization_barrier((proj_loc[0], small, token, g1, local2, local3))
         g2 = gather(local2)
-        g3 = gather(lax.optimization_barrier((w_down[1], local2))[0])
+        g3 = gather(lax.optimization_barrier((local3, local2))[0])
+        g0, small = gather_first(tp, fs // 2, (proj0,), small, (((0, None, 0, TILE, 0),),), 0, 1)
         qkv_at = [(g1, ff_tiles + wide_tiles), (g2, ff_tiles)]
-        proj_at = [(g1, ff_tiles + wide_tiles + qkv_tiles), (g2, ff_tiles + qkv_tiles)]
+        proj_at = [(g0, 0), (g2, ff_tiles + qkv_tiles)]
         down_at = [(g1, ff_tiles), (g3, 0)]
 
         small = small.reshape(2, tp, fs // 2, -1).transpose(1, 2, 0, 3).reshape(tp, fs, -1)
@@ -421,7 +426,6 @@
         qkv_bias = small[..., cuts[2]:cuts[3]].reshape(tp, fs, n_layers, 3, piece).transpose(2, 0, 3, 1, 4).reshape(n_layers, -1)
         up_bias = small[..., cuts[3]:cuts[4]].reshape(tp, fs, n_layers, -1).transpose(2, 0, 1, 3).reshape(n_layers, -1)
 
-        current = lax.dynamic_slice_in_dim(hidden, me * my_seqs, my_seqs, 0).reshape(my_seqs * seq_len, d_model)
         lens = lax.dynamic_slice_in_dim(seq_lens, me * my_seqs, my_seqs, 0)
 
         for l in range(n_layers):

time: 771 us -> 787 us (1.021)
  Pallas kernels: 633 us -> 662 us
  waiting for transfers between devices: 88 us -> 80.1 us
    pallas_call x1 -> x2, Pallas kernels: 273 us -> 301 us  [gather_first(): pl.pallas_call(functools.partial(gather_kernel, ny, nx, loads, len(arrays...]
    all_gather x2, waiting for transfers between devices: 8.2 us -> 0.01 us  [gather(): lax.all_gather(with_layout_constraint(x, Layout(major_to_minor=tuple(rang...]
  transfers between devices with their start and end apart: 14 -> 14, of which waited for: 8 -> 6; matrix products, arithmetic and copies ran while one was open for 2% -> 1% of each run, Pallas kernels for 45% -> 51%
where the time goes in v3:
time: 787 us; the launch traced here: 786 us
  Pallas kernels  662 us (84%)
  waiting for transfers between devices  80.1 us (10%)
  local copies, waits for them, and re-layouts  17 us (2%)
  between operations  13.7 us (2%)
  starting transfers between devices  10.4 us (1%)
    pallas_call x2, Pallas kernels, gather_first(): pl.pallas_call(functools.partial(gather_kernel, ny, nx, loads, len(arrays...  301 us
    pallas_call x11, Pallas kernels, matmul(): pl.pallas_call(functools.partial(mm_kernel, relu, steps, resid is not Non...  295 us
    pallas_call x2, Pallas kernels, attend(): pl.pallas_call(functools.partial(attn_kernel, head_dim, block // head_dim...  57.7 us
    ppermute x4, waiting for transfers between devices, per_device(): left = lax.ppermute(own, 'tp', minus)  42 us
    ppermute x4, waiting for transfers between devices, per_device(): blocks.append((2, j, lax.ppermute(here[2], 'tp', perm)))  37.4 us
  transfers between devices with their start and end apart: 14, of which 6 were waited for; matrix products, arithmetic and copies ran while one was open for 1% of the time, Pallas kernels for 51%

profile of v3, /device:TPU:97, one launch (start us, length us, event | category | flops | bytes accessed | tf_op | source)
XLA Modules:
  0.0 785.6 jit_solution(13219341889463376917)
XLA Ops:
  6.6 1.5 fusion.1
  8.0 1.2 copy.30.refs_2_
  9.2 1.1 copy.31.refs_3_
  10.3 1.1 fusion.2
  11.4 0.2 reshape_squeeze.35
  11.6 0.8 copy.29
  12.3 0.2 reshape_squeeze.36
  12.5 0.7 copy.32
  13.3 0.7 copy.42
  14.0 0.7 convert_bitcast_fusion
  14.7 0.7 copy.33
  15.3 0.1 reshape.97
  15.4 0.7 convert_bitcast_fusion.1
  16.1 0.6 fusion.refs_1_
  16.7 0.6 broadcast_in_dim.3.refs_6_
  17.3 249.7 %shard_map.100 = (bf16[32,256,5632]{2,1,0:T(8,128)(2,1)}, f32[2,4,4,8,128]{4,3,2,1,0:T(8,128)}, bf16[256,4096]{1,0:T(8,128)(2,1)}, bf16[256,2048]{1,0:T(8,128)(2,1)}, bf16[1024,2048]{1,0:T(8,128)(2,1)}) custom-call(bf16[2,256,2048]{2,1,0:T(8,128)(2,1)} %refs_0_.1, bf16[2,256,2048]{2,1,0:T(8,128)(2,1)} %refs_1_.1, bf16[256,1536]{1,0:T(8,128)(2,1)} %copy.30.refs_2_, ...), custom_call_target="tpu_custom_call" | custom-call | flops 738197504 | bytes 184549376 | tf_op jit(solution)/shard_map/pallas_call | solution.py:363
  267.2 0.7 all-gather.7.cloned.1.call-update
  267.9 51.8 %shard_map.101 = (bf16[32,256,512]{2,1,0:T(8,128)(2,1)}, f32[2,4,4,32,128]{4,3,2,1,0:T(8,128)}) custom-call(bf16[256,512]{1,0:T(8,128)(2,1)} %bitcast.81, f32[32,128]{1,0:T(8,128)} %fusion.refs_1_), custom_call_target="tpu_custom_call" | custom-call | flops 67108864 | bytes 16777216 | tf_op jit(solution)/shard_map/pallas_call | solution.py:363
  319.7 1.2 reshape.83
  320.9 0.3 copy.34
  321.3 0.2 slice_reduce_fusion
  321.5 0.1 reshape.85
  321.7 0.7 slice.81.b_ref
  322.6 0.7 slice.92.b_ref
  323.3 0.6 dynamic_slice.3.lens_ref
  323.9 0.7 fusion.4
  324.6 0.6 slice_bitcast_fusion.4
  325.2 0.6 slice_bitcast_fusion
  325.9 35.9 %shard_map.102 = bf16[1024,6144]{1,0:T(8,128)(2,1)} custom-call(bf16[1024,2048]{1,0:T(8,128)(2,1)} %get-tuple-element.17.x_ref.refs_0_, bf16[32,256,5632]{2,1,0:T(8,128)(2,1)} %get-tuple-element.21.w_ref, f32[1,6144]{1,0:T(1,128)} %slice.81.b_ref, f32[2,2048]{1,0:T(2,128)} %get-tuple-element.38.refs_0_), custom_call_target="tpu_custom_call" | custom-call | flops 25769803776 | bytes 41943040 | tf_op jit(solution)/shard_map/pallas_call | solution.py:142
  361.7 28.9 %shard_map.103 = bf16[2,512,2048]{2,1,0:T(8,128)(2,1)} custom-call(s32[2]{0:T(128)} %dynamic_slice.3.lens_ref, bf16[2,512,6144]{2,1,0:T(8,128)(2,1)} %bitcast.74, bf16[2,512,6144]{2,1,0:T(8,128)(2,1)} %bitcast.75, bf16[2,512,6144]{2,1,0:T(8,128)(2,1)} %bitcast.76), custom_call_target="tpu_custom_call" | custom-call | flops 17179869184 | bytes 16777216 | tf_op jit(solution)/shard_map/pallas_call | solution.py:67
  390.6 13.6 %shard_map.104.x_ref.refs_0_ = bf16[1024,2048]{1,0:T(8,128)(2,1)} custom-call(bf16[1024,2048]{1,0:T(8,128)(2,1)} %bitcast.99, bf16[32,256,512]{2,1,0:T(8,128)(2,1)} %get-tuple-element.25.w_ref, f32[1,2048]{1,0:T(1,128)} %get-tuple-element.44.b_ref, bf16[1024,2048]{1,0:T(8,128)(2,1)} %get-tuple-element.17.x_ref.refs_0_), custom_call_target="tpu_custom_call" | custom-call | flops 8589934592 | bytes 16777216 | tf_op jit(solution)/shard_map/pallas_call | solution.py:142
  404.2 46.1 %shard_map.105.x_ref = bf16[1024,8192]{1,0:T(8,128)(2,1)} custom-call(bf16[1024,2048]{1,0:T(8,128)(2,1)} %shard_map.104.x_ref.refs_0_, bf16[32,256,5632]{2,1,0:T(8,128)(2,1)} %get-tuple-element.21.w_ref, f32[1,8192]{1,0:T(1,128)} %bitcast.92, f32[2,2048]{1,0:T(2,128)} %get-tuple-element.37.refs_0_), custom_call_target="tpu_custom_call" | custom-call | flops 34359738368 | bytes 54525952 | tf_op jit(solution)/shard_map/pallas_call | solution.py:142
  450.3 48.9 %shard_map.106.x_ref.refs_0_ = bf16[1024,2048]{1,0:T(8,128)(2,1)} custom-call(bf16[1024,8192]{1,0:T(8,128)(2,1)} %shard_map.105.x_ref, bf16[32,256,5632]{2,1,0:T(8,128)(2,1)} %get-tuple-element.21.w_ref, f32[1,2048]{1,0:T(1,128)} %get-tuple-element.43.b_ref, bf16[1024,2048]{1,0:T(8,128)(2,1)} %shard_map.104.x_ref.refs_0_), custom_call_target="tpu_custom_call" | custom-call | flops 34359738368 | bytes 54525952 | tf_op jit(solution)/shard_map/pallas_call | solution.py:142
  499.2 35.8 %shard_map.107 = bf16[1024,6144]{1,0:T(8,128)(2,1)} custom-call(bf16[1024,2048]{1,0:T(8,128)(2,1)} %shard_map.106.x_ref.refs_0_, bf16[32,256,4096]{2,1,0:T(8,128)(2,1)} %bitcast.22.w_ref, f32[1,6144]{1,0:T(1,128)} %slice.92.b_ref, f32[2,2048]{1,0:T(2,128)} %get-tuple-element.36.refs_0_), custom_call_target="tpu_custom_call" | custom-call | flops 25769803776 | bytes 41943040 | tf_op jit(solution)/shard_map/pallas_call | solution.py:142
  535.0 28.8 %shard_map.108 = bf16[2,512,2048]{2,1,0:T(8,128)(2,1)} custom-call(s32[2]{0:T(128)} %dynamic_slice.3.lens_ref, bf16[2,512,6144]{2,1,0:T(8,128)(2,1)} %bitcast.96, bf16[2,512,6144]{2,1,0:T(8,128)(2,1)} %bitcast.97, bf16[2,512,6144]{2,1,0:T(8,128)(2,1)} %bitcast.98), custom_call_target="tpu_custom_call" | custom-call | flops 17179869184 | bytes 16777216 | tf_op jit(solution)/shard_map/pallas_call | solution.py:67
  563.8 13.8 %shard_map.109.x_ref.refs_0_ = bf16[1024,2048]{1,0:T(8,128)(2,1)} custom-call(bf16[1024,2048]{1,0:T(8,128)(2,1)} %bitcast.77, bf16[32,256,4096]{2,1,0:T(8,128)(2,1)} %bitcast.22.w_ref, f32[1,2048]{1,0:T(1,128)} %get-tuple-element.42.b_ref, bf16[1024,2048]{1,0:T(8,128)(2,1)} %shard_map.106.x_ref.refs_0_), custom_call_target="tpu_custom_call" | custom-call | flops 8589934592 | bytes 16777216 | tf_op jit(solution)/shard_map/pallas_call | solution.py:142
  577.6 45.4 %shard_map.110.x_ref = bf16[1024,8192]{1,0:T(8,128)(2,1)} custom-call(bf16[1024,2048]{1,0:T(8,128)(2,1)} %shard_map.109.x_ref.refs_0_, bf16[32,256,4096]{2,1,0:T(8,128)(2,1)} %bitcast.22.w_ref, f32[1,8192]{1,0:T(1,128)} %bitcast.91, f32[2,2048]{1,0:T(2,128)} %get-tuple-element.35.refs_0_), custom_call_target="tpu_custom_call" | custom-call | flops 34359738368 | bytes 54525952 | tf_op jit(solution)/shard_map/pallas_call | solution.py:142
  623.0 2.2 copy-done
  625.2 13.9 %shard_map.113.refs_0_ = bf16[1024,512]{1,0:T(8,128)(2,1)S(1)} custom-call(bf16[1024,8192]{1,0:T(8,128)(2,1)} %shard_map.110.x_ref, bf16[32,256,2048]{2,1,0:T(8,128)(2,1)} %bitcast.69, f32[1,2048]{1,0:T(1,128)S(1)} %get-tuple-element.41.b_ref, bf16[1024,2048]{1,0:T(8,128)(2,1)S(1)} %copy-done), custom_call_target="tpu_custom_call" | custom-call | flops 8589934592 | bytes 26214400 | tf_op jit(solution)/shard_map/pallas_call | solution.py:142
  639.1 0.1 collective-permute-start.10
  639.2 1.4 collective-permute-start.4
  640.7 13.9 %shard_map.111.refs_3_ = bf16[1024,512]{1,0:T(8,128)(2,1)S(1)} custom-call(bf16[1024,8192]{1,0:T(8,128)(2,1)} %shard_map.110.x_ref, bf16[32,256,2048]{2,1,0:T(8,128)(2,1)} %bitcast.70, f32[1,2048]{1,0:T(1,128)S(1)} %get-tuple-element.41.b_ref, bf16[1024,2048]{1,0:T(8,128)(2,1)S(1)} %copy-done), custom_call_target="tpu_custom_call" | custom-call | flops 8589934592 | bytes 26214400 | tf_op jit(solution)/shard_map/pallas_call | solution.py:142
  654.6 0.3 collective-permute-start
  654.9 2.5 collective-permute-start.11
  657.4 13.9 %shard_map.114.refs_0_ = bf16[1024,512]{1,0:T(8,128)(2,1)S(1)} custom-call(bf16[1024,8192]{1,0:T(8,128)(2,1)} %shard_map.110.x_ref, bf16[32,256,2048]{2,1,0:T(8,128)(2,1)} %bitcast.71, f32[1,2048]{1,0:T(1,128)S(1)} %get-tuple-element.41.b_ref, bf16[1024,2048]{1,0:T(8,128)(2,1)S(1)} %copy-done), custom_call_target="tpu_custom_call" | custom-call | flops 8589934592 | bytes 26214400 | tf_op jit(solution)/shard_map/pallas_call | solution.py:142
  671.3 0.2 collective-permute-start.6
  671.5 13.9 %shard_map.112.refs_3_ = bf16[1024,512]{1,0:T(8,128)(2,1)S(1)} custom-call(bf16[1024,8192]{1,0:T(8,128)(2,1)} %shard_map.110.x_ref, bf16[32,256,2048]{2,1,0:T(8,128)(2,1)} %bitcast.72, f32[1,2048]{1,0:T(1,128)S(1)} %get-tuple-element.41.b_ref, bf16[1024,2048]{1,0:T(8,128)(2,1)S(1)} %copy-done), custom_call_target="tpu_custom_call" | custom-call | flops 8589934592 | bytes 26214400 | tf_op jit(solution)/shard_map/pallas_call | solution.py:142
  685.4 0.1 collective-permute-start.2
  685.6 1.4 collective-permute-start.8
  687.0 1.3 collective-permute-start.9
  688.3 21.0 %collective-permute-done.6.refs_2_ = bf16[1024,512]{1,0:T(8,128)(2,1)S(1)} collective-permute-done((bf16[1024,512]{1,0:T(8,128)(2,1)S(1)}, bf16[1024,512]{1,0:T(8,128)(2,1)S(1)}, u32[]{:S(2)}, u32[]{:S(2)}) %collective-permute-start.6) | collective-permute-done | bytes 1048608 | tf_op jit(solution)/shard_map/ppermute | solution.py:450
  709.3 1.2 collective-permute-start.7
  710.5 0.2 collective-permute-start.5
  710.8 21.0 %collective-permute-done.2.refs_5_ = bf16[1024,512]{1,0:T(8,128)(2,1)S(1)} collective-permute-done((bf16[1024,512]{1,0:T(8,128)(2,1)S(1)}, bf16[1024,512]{1,0:T(8,128)(2,1)S(1)}, u32[]{:S(2)}, u32[]{:S(2)}) %collective-permute-start.2) | collective-permute-done | bytes 1048608 | tf_op jit(solution)/shard_map/ppermute | solution.py:450
  731.8 1.2 collective-permute-start.3
  733.0 0.2 collective-permute-start.1
  733.2 2.7 shard_map.115.refs_6_
  736.0 2.7 shard_map.116.refs_2_
  738.7 15.5 %collective-permute-done.7.refs_1_ = bf16[1024,512]{1,0:T(8,128)(2,1)S(1)} collective-permute-done((bf16[1024,512]{1,0:T(8,128)(2,1)S(1)}, bf16[1024,512]{1,0:T(8,128)(2,1)S(1)}, u32[]{:S(2)}, u32[]{:S(2)}) %collective-permute-start.7) | collective-permute-done | bytes 1048608 | tf_op jit(solution)/shard_map/ppermute | solution.py:454
  754.2 0.7 collective-permute-done.5.refs_0_
  754.9 1.3 shard_map.117.refs_2_
  756.3 19.5 %collective-permute-done.3.refs_1_ = bf16[1024,512]{1,0:T(8,128)(2,1)S(1)} collective-permute-done((bf16[1024,512]{1,0:T(8,128)(2,1)S(1)}, bf16[1024,512]{1,0:T(8,128)(2,1)S(1)}, u32[]{:S(2)}, u32[]{:S(2)}) %collective-permute-start.3) | collective-permute-done | bytes 1048608 | tf_op jit(solution)/shard_map/ppermute | solution.py:454
  775.8 1.6 collective-permute-done.1.refs_0_
  777.4 1.3 shard_map.118
  (27 shorter events, 0.4 us)
Async XLA Ops:
  6.5 492.7 %all-gather.5.cloned.1.call-start = ((), (), s32[]{:S(2)}) async-start(), calls=%async_computation | async-start | bytes 69206016 | tf_op jit(solution)/shard_map/all_gather | solution.py:390
  17.3 306.0 %copy-start.1 = (s32[8]{0:T(128)S(1)}, s32[8]{0:T(128)}, u32[]{:S(2)}) copy-start(s32[8]{0:T(128)} %param.11) | copy-start | bytes 100
  267.1 355.9 %all-gather.7.cloned.1.call-start = ((), (), s32[]{:S(2)}) async-start(), calls=%async_computation.1 | async-start | bytes 34603008 | tf_op jit(solution)/shard_map/all_gather | solution.py:390
  623.0 2.2 copy-start
  639.1 46.3 %collective-permute-start.10 = (bf16[1024,512]{1,0:T(8,128)(2,1)S(1)}, bf16[1024,512]{1,0:T(8,128)(2,1)S(1)}, u32[]{:S(2)}, u32[]{:S(2)}) collective-permute-start(bf16[1024,512]{1,0:T(8,128)(2,1)S(1)} %shard_map.113.refs_0_), channel_id=1, source_target_pairs={{0,24},{8,0},{16,8},{24,16},{1,25},{9,1},{17,9},{25,17},{2,26},{10... | collective-permute-start | bytes 3145736 | tf_op jit(solution)/shard_map/ppermute | solution.py:450
  639.2 46.4 %collective-permute-start.4 = (bf16[1024,512]{1,0:T(8,128)(2,1)S(1)}, bf16[1024,512]{1,0:T(8,128)(2,1)S(1)}, u32[]{:S(2)}, u32[]{:S(2)}) collective-permute-start(bf16[1024,512]{1,0:T(8,128)(2,1)S(1)} %shard_map.113.refs_0_), channel_id=1, source_target_pairs={{0,8},{8,16},{16,24},{24,0},{1,9},{9,17},{17,25},{25,1},{2,10},{10... | collective-permute-start | bytes 3145736 | tf_op jit(solution)/shard_map/ppermute | solution.py:449
  654.6 32.4 %collective-permute-start = (bf16[1024,512]{1,0:T(8,128)(2,1)S(1)}, bf16[1024,512]{1,0:T(8,128)(2,1)S(1)}, u32[]{:S(2)}, u32[]{:S(2)}) collective-permute-start(bf16[1024,512]{1,0:T(8,128)(2,1)S(1)} %shard_map.111.refs_3_), channel_id=1, source_target_pairs={{0,8},{8,16},{16,24},{24,0},{1,9},{9,17},{17,25},{25,1},{2,10},{10... | collective-permute-start | bytes 3145736 | tf_op jit(solution)/shard_map/ppermute | solution.py:449
  654.9 55.7 %collective-permute-start.11 = (bf16[1024,512]{1,0:T(8,128)(2,1)S(1)}, bf16[1024,512]{1,0:T(8,128)(2,1)S(1)}, u32[]{:S(2)}, u32[]{:S(2)}) collective-permute-start(bf16[1024,512]{1,0:T(8,128)(2,1)S(1)} %shard_map.111.refs_3_), channel_id=1, source_target_pairs={{0,24},{8,0},{16,8},{24,16},{1,25},{9,1},{17,9},{25,17},{2,26},{10... | collective-permute-start | bytes 3145736 | tf_op jit(solution)/shard_map/ppermute | solution.py:450
  671.3 38.0 %collective-permute-start.6 = (bf16[1024,512]{1,0:T(8,128)(2,1)S(1)}, bf16[1024,512]{1,0:T(8,128)(2,1)S(1)}, u32[]{:S(2)}, u32[]{:S(2)}) collective-permute-start(bf16[1024,512]{1,0:T(8,128)(2,1)S(1)} %shard_map.114.refs_0_), channel_id=1, source_target_pairs={{0,24},{8,0},{16,8},{24,16},{1,25},{9,1},{17,9},{25,17},{2,26},{10... | collective-permute-start | bytes 3145736 | tf_op jit(solution)/shard_map/ppermute | solution.py:450
  685.4 46.3 %collective-permute-start.2 = (bf16[1024,512]{1,0:T(8,128)(2,1)S(1)}, bf16[1024,512]{1,0:T(8,128)(2,1)S(1)}, u32[]{:S(2)}, u32[]{:S(2)}) collective-permute-start(bf16[1024,512]{1,0:T(8,128)(2,1)S(1)} %shard_map.112.refs_3_), channel_id=1, source_target_pairs={{0,24},{8,0},{16,8},{24,16},{1,25},{9,1},{17,9},{25,17},{2,26},{10... | collective-permute-start | bytes 3145736 | tf_op jit(solution)/shard_map/ppermute | solution.py:450
  685.6 47.4 %collective-permute-start.8 = (bf16[1024,512]{1,0:T(8,128)(2,1)S(1)}, bf16[1024,512]{1,0:T(8,128)(2,1)S(1)}, u32[]{:S(2)}, u32[]{:S(2)}) collective-permute-start(bf16[1024,512]{1,0:T(8,128)(2,1)S(1)} %shard_map.114.refs_0_), channel_id=1, source_target_pairs={{0,8},{8,16},{16,24},{24,0},{1,9},{9,17},{17,25},{25,1},{2,10},{10... | collective-permute-start | bytes 3145736 | tf_op jit(solution)/shard_map/ppermute | solution.py:449
  687.0 49.0 %collective-permute-start.9 = (bf16[1024,512]{1,0:T(8,128)(2,1)S(1)}, bf16[1024,512]{1,0:T(8,128)(2,1)S(1)}, u32[]{:S(2)}, u32[]{:S(2)}) collective-permute-start(bf16[1024,512]{1,0:T(8,128)(2,1)S(1)} %shard_map.112.refs_3_), channel_id=1, source_target_pairs={{0,8},{8,16},{16,24},{24,0},{1,9},{9,17},{17,25},{25,1},{2,10},{10... | collective-permute-start | bytes 3145736 | tf_op jit(solution)/shard_map/ppermute | solution.py:449
  709.3 44.9 %collective-permute-start.7 = (bf16[1024,512]{1,0:T(8,128)(2,1)S(1)}, bf16[1024,512]{1,0:T(8,128)(2,1)S(1)}, u32[]{:S(2)}, u32[]{:S(2)}) collective-permute-start(bf16[1024,512]{1,0:T(8,128)(2,1)S(1)} %collective-permute-done.6.refs_2_), channel_id=1, source_target_pairs={{0,24},{8,0},{16,8},{24,16},{1,25},{9,1},{17,9},{25,17},{2,26},{10... | collective-permute-start | bytes 3145736 | tf_op jit(solution)/shard_map/ppermute | solution.py:454
  710.5 44.4 %collective-permute-start.5 = (bf16[1024,512]{1,0:T(8,128)(2,1)S(1)}, bf16[1024,512]{1,0:T(8,128)(2,1)S(1)}, u32[]{:S(2)}, u32[]{:S(2)}) collective-permute-start(bf16[1024,512]{1,0:T(8,128)(2,1)S(1)} %collective-permute-done.4.refs_1_), channel_id=1, source_target_pairs={{0,8},{8,16},{16,24},{24,0},{1,9},{9,17},{17,25},{25,1},{2,10},{10... | collective-permute-start | bytes 3145736 | tf_op jit(solution)/shard_map/ppermute | solution.py:454
  731.8 44.0 %collective-permute-start.3 = (bf16[1024,512]{1,0:T(8,128)(2,1)S(1)}, bf16[1024,512]{1,0:T(8,128)(2,1)S(1)}, u32[]{:S(2)}, u32[]{:S(2)}) collective-permute-start(bf16[1024,512]{1,0:T(8,128)(2,1)S(1)} %collective-permute-done.2.refs_5_), channel_id=1, source_target_pairs={{0,24},{8,0},{16,8},{24,16},{1,25},{9,1},{17,9},{25,17},{2,26},{10... | collective-permute-start | bytes 3145736 | tf_op jit(solution)/shard_map/ppermute | solution.py:454
  733.0 44.4 %collective-permute-start.1 = (bf16[1024,512]{1,0:T(8,128)(2,1)S(1)}, bf16[1024,512]{1,0:T(8,128)(2,1)S(1)}, u32[]{:S(2)}, u32[]{:S(2)}) collective-permute-start(bf16[1024,512]{1,0:T(8,128)(2,1)S(1)} %collective-permute-done.refs_4_), channel_id=1, source_target_pairs={{0,8},{8,16},{16,24},{24,0},{1,9},{9,17},{17,25},{25,1},{2,10},{10... | collective-permute-start | bytes 3145736 | tf_op jit(solution)/shard_map/ppermute | solution.py:454
Sparse Core Ops, SparseCore 0:
  267.2 209.6 all-gather.4
  478.9 107.5 all-gather.6
